TPU v7x, 32 devices: a whole 2x2x4 slice. The times are simulated.
32 devices in a mesh: row: 8 (over z, x), col: 4 (over y, core).
Axes of the slice: x: 2, y: 2, z: 4, core: 2. Of those that a mesh axis runs over, the one named last changes fastest.
Arguments:
- hub_seeds: bfloat16 [192, 64, 128], P('row'), may hold values from -6 to 6
- tile_blocks: bfloat16 [8192, 128, 128], P(('row', 'col')), may hold values from -8 to 8
- tile_rows: int32 [8192], P(('row', 'col')), may hold values from 0 to 127, as said below
- tile_cols: int32 [8192], P(('row', 'col')), may hold values from 0 to 127, as said below
- tile_count: int32 [32], P(('row', 'col')), may hold values from 64 to 256, as said below
- row_blocks: int32 [8], replicated, may hold values from 8 to 24, as said below
Outputs:
- authority: bfloat16 [128, 64, 128], P(('row', 'col'))
- hub_scores: bfloat16 [192, 64, 128], P('row')
Inputs may be any that keep to these rules, and one draw needn't show every extreme that they name: Row range r covers row blocks starts[r] to starts[r] + row_blocks[r] - 1, the ranges in order and together all 128 blocks; the longest range has exactly 24 blocks in every draw. `tile_rows`: every tile of a device lies in the row range of the device's row index; no pair of row block and column block repeats within a device. `tile_cols`: A device with column index c holds only column blocks b with (b // 4) % 4 == c. The live tiles of a device are its first tile_count slots; some device has all 256 slots live in every draw.
All inputs are finite; a program needn't handle non-finite values.
Results may differ from a plain program's by a relative error of at most 0.02.
Values may be sent and summed in bfloat16 or wider, within the bound.
A program may use at most 192 MiB of HBM per device.

v0:
```python
import jax
import jax.numpy as jnp
from jax import lax
from jax.sharding import PartitionSpec as P

ITERS = 2
RB_DEV = 16


def local(hub_seeds, tile_blocks, tile_rows, tile_cols, tile_count, row_blocks):
    own_row = lax.axis_index("row")
    row_devs = lax.axis_size("row")
    col_devs = lax.axis_size("col")
    slot_count = hub_seeds.shape[0]
    tile_side = tile_blocks.shape[1]
    tile_slots = tile_blocks.shape[0]
    group_len = RB_DEV // col_devs
    set_blocks = group_len * row_devs
    host_count = RB_DEV * row_devs * tile_side
    span_length = row_blocks[own_row]
    before = jnp.arange(row_devs, dtype=jnp.int32) < own_row
    first_block = jnp.sum(jnp.where(before, row_blocks, 0))
    live_tile = jnp.arange(tile_slots, dtype=jnp.int32) < tile_count[0]
    row_slot = jnp.where(live_tile, tile_rows - first_block, slot_count)
    col_slot = jnp.where(
        live_tile,
        tile_cols // group_len // col_devs * group_len + tile_cols % group_len,
        set_blocks,
    )
    row_pick = jnp.clip(row_slot, 0, slot_count - 1)
    col_pick = jnp.clip(col_slot, 0, set_blocks - 1)
    usable = jnp.arange(slot_count, dtype=jnp.int32) < span_length
    hub_now = jnp.where(usable[:, None, None], hub_seeds, jnp.zeros_like(hub_seeds))
    authority = None
    for iteration in range(ITERS):
        picked = jnp.take(hub_now, row_pick, axis=0, mode="clip")
        products = jnp.einsum(
            "tkr,trc->tkc", picked, tile_blocks, preferred_element_type=jnp.float32
        )
        set_terms = jax.ops.segment_sum(products, col_slot, num_segments=set_blocks, mode="drop")
        raw_set = lax.psum(set_terms.astype(jnp.bfloat16), "row").astype(jnp.float32)
        squares = lax.psum(jnp.sum(raw_set * raw_set, axis=(0, 2)), "col")
        factor = 1.0 / jnp.sqrt(squares / host_count + 1.0)
        column_set = (raw_set * factor[None, :, None]).astype(jnp.bfloat16)
        authority = lax.dynamic_slice_in_dim(column_set, own_row * group_len, group_len, 0)
        picked_cols = jnp.take(column_set, col_pick, axis=0, mode="clip")
        back_products = jnp.einsum(
            "tkc,trc->tkr", picked_cols, tile_blocks, preferred_element_type=jnp.float32
        )
        hub_terms = jax.ops.segment_sum(
            back_products, row_slot, num_segments=slot_count, mode="drop"
        )
        raw_hub = lax.psum(hub_terms.astype(jnp.bfloat16), "col").astype(jnp.float32)
        squares = lax.psum(jnp.sum(raw_hub * raw_hub, axis=(0, 2)), "row")
        factor = 1.0 / jnp.sqrt(squares / host_count + 1.0)
        hub_now = (raw_hub * factor[None, :, None]).astype(jnp.bfloat16)
    return (authority, hub_now)


def solution(mesh):
    return jax.shard_map(
        local,
        mesh=mesh,
        in_specs=(
            P("row", None, None),
            P(("row", "col"), None, None),
            P(("row", "col")),
            P(("row", "col")),
            P(("row", "col")),
            P(),
        ),
        out_specs=(P(("row", "col"), None, None), P("row", None, None)),
        check_vma=False,
    )
```

profile of v0, /device:TPU:0, one launch (start us, length us, event | category | flops | bytes accessed | tf_op | source)
XLA Modules:
  0.0 463.5 jit_solution(11632191388393047059)
XLA Ops:
  7.2 0.0 all-reduce.5.cloned.1.call-start
  7.2 1.3 fusion.10
  8.5 1.2 dynamic_slice.6
  9.7 0.6 iota_compare_fusion.1
  11.0 1.4 broadcast_clamp_fusion
  12.4 1.1 broadcast_select_fusion
  13.5 3.1 gather_fusion
  16.6 10.2 %fusion.12 = f32[256,64,128]{2,1,0:T(8,128)} fusion(bf16[256,64,128]{2,1,0:T(8,128)(2,1)} %gather_fusion, bf16[256,128,128]{2,1,0:T(8,128)(2,1)} %param.7), kind=kOutput, calls=%fused_computation.50 | convolution fusion | flops 536870912 | bytes 20971520 | tf_op jit(solution)/shard_map/tkr,trc->tkc/dot_general | solution.py:37
  26.8 0.1 broadcast.40.clone
  26.9 26.3 %scatter_fusion = f32[32,64,128]{2,1,0:T(8,128)S(1)} fusion(f32[32,64,128]{2,1,0:T(8,128)S(1)} %broadcast.40.clone, s32[256]{0:T(256)S(1)} %get-tuple-element.3, f32[256,64,128]{2,1,0:T(8,128)} %fusion.12), kind=kCustom, calls=%fused_computation.4 | custom fusion | flops 2097152 | bytes 25166848 | tf_op jit(solution)/shard_map/scatter-add | solution.py:40
  53.2 0.9 convert_element_type.36
  54.1 0.0 all-reduce.5.cloned.1.call-update
  54.2 0.0 all-reduce.7.cloned.1.call-start
  54.2 75.5 %all-reduce.5.cloned.1.call-done = bf16[32,64,128]{2,1,0:T(8,128)(2,1)} async-done(((bf16[32,64,128]{2,1,0:T(8,128)(2,1)}), bf16[32,64,128]{2,1,0:T(8,128)(2,1)}) %all-reduce.5.cloned.1.call-update) | async-done | bytes 524304 | tf_op jit(solution)/shard_map/psum | solution.py:41
  129.8 1.3 fusion
  131.0 5.7 %psum.57 = f32[64]{0:T(128)S(1)} all-reduce(f32[64]{0:T(128)S(1)} %fusion), channel_id=1, replica_groups=mesh['row'=8,'col'=4] {'col'}, use_global_device_ids=true, to_apply=%region_4.5 | all-reduce | flops 64 | bytes 512 | tf_op jit(solution)/shard_map/psum | solution.py:42
  136.7 1.3 fusion.1
  138.0 3.1 gather_fusion.1
  141.0 13.7 %fusion.13 = f32[256,64,128]{2,1,0:T(8,128)} fusion(bf16[256,64,128]{2,1,0:T(8,128)(2,1)} %gather_fusion.1, bf16[256,128,128]{2,1,0:T(8,128)(2,1)} %param.7), kind=kOutput, calls=%fused_computation.51 | convolution fusion | flops 536870912 | bytes 20971520 | tf_op jit(solution)/shard_map/tkc,trc->tkr/dot_general | solution.py:47
  154.8 0.1 broadcast.42.clone
  154.8 26.3 %scatter_fusion.1 = f32[24,64,128]{2,1,0:T(8,128)S(1)} fusion(f32[24,64,128]{2,1,0:T(8,128)S(1)} %broadcast.42.clone, s32[256]{0:T(256)S(1)} %get-tuple-element.7, f32[256,64,128]{2,1,0:T(8,128)} %fusion.13), kind=kCustom, calls=%fused_computation.5 | custom fusion | flops 2097152 | bytes 25166848 | tf_op jit(solution)/shard_map/scatter-add | solution.py:50
  181.1 0.8 convert_element_type.39
  181.9 0.0 all-reduce.7.cloned.1.call-update
  182.0 0.0 all-reduce.9.cloned.1.call-start
  182.0 32.3 %all-reduce.7.cloned.1.call-done = bf16[24,64,128]{2,1,0:T(8,128)(2,1)} async-done(((bf16[24,64,128]{2,1,0:T(8,128)(2,1)}), bf16[24,64,128]{2,1,0:T(8,128)(2,1)}) %all-reduce.7.cloned.1.call-update) | async-done | bytes 393232 | tf_op jit(solution)/shard_map/psum | solution.py:53
  214.3 1.2 fusion.4
  215.5 21.5 %psum.59 = f32[64]{0:T(128)S(1)} all-reduce(f32[64]{0:T(128)S(1)} %fusion.4), channel_id=1, replica_groups=mesh['row'=8,'col'=4] {'row'}, use_global_device_ids=true, to_apply=%region_8.9 | all-reduce | flops 64 | bytes 512 | tf_op jit(solution)/shard_map/psum | solution.py:54
  237.1 1.2 fusion.5
  238.2 3.1 gather_fusion.2
  241.3 10.2 %fusion.14 = f32[256,64,128]{2,1,0:T(8,128)} fusion(bf16[256,64,128]{2,1,0:T(8,128)(2,1)} %gather_fusion.2, bf16[256,128,128]{2,1,0:T(8,128)(2,1)} %param.7), kind=kOutput, calls=%fused_computation.52 | convolution fusion | flops 536870912 | bytes 20971520 | tf_op jit(solution)/shard_map/tkr,trc->tkc/dot_general | solution.py:37
  251.5 0.1 broadcast.40
  251.6 26.3 %scatter_fusion.2 = f32[32,64,128]{2,1,0:T(8,128)S(1)} fusion(f32[32,64,128]{2,1,0:T(8,128)S(1)} %broadcast.40, s32[256]{0:T(256)S(1)} %get-tuple-element.3, f32[256,64,128]{2,1,0:T(8,128)} %fusion.14), kind=kCustom, calls=%fused_computation.6 | custom fusion | flops 2097152 | bytes 25166848 | tf_op jit(solution)/shard_map/scatter-add | solution.py:40
  277.9 0.9 convert_element_type.42
  278.9 0.0 all-reduce.11.cloned.1.call-start
  278.9 69.0 %all-reduce.9.cloned.1.call-done = bf16[32,64,128]{2,1,0:T(8,128)(2,1)} async-done(((bf16[32,64,128]{2,1,0:T(8,128)(2,1)}), bf16[32,64,128]{2,1,0:T(8,128)(2,1)}) %all-reduce.9.cloned.1.call-update) | async-done | bytes 524304 | tf_op jit(solution)/shard_map/psum | solution.py:41
  347.9 1.3 fusion.2
  349.2 5.7 %psum.61 = f32[64]{0:T(128)S(1)} all-reduce(f32[64]{0:T(128)S(1)} %fusion.2), channel_id=1, replica_groups=mesh['row'=8,'col'=4] {'col'}, use_global_device_ids=true, to_apply=%region_12.13 | all-reduce | flops 64 | bytes 512 | tf_op jit(solution)/shard_map/psum | solution.py:42
  354.9 1.3 fusion.3
  356.1 3.1 gather_fusion.3
  359.2 13.7 %fusion.15 = f32[256,64,128]{2,1,0:T(8,128)} fusion(bf16[256,64,128]{2,1,0:T(8,128)(2,1)} %gather_fusion.3, bf16[256,128,128]{2,1,0:T(8,128)(2,1)} %param.7), kind=kOutput, calls=%fused_computation.53 | convolution fusion | flops 536870912 | bytes 20971520 | tf_op jit(solution)/shard_map/tkc,trc->tkr/dot_general | solution.py:47
  372.9 0.1 broadcast.42
  373.0 26.3 %scatter_fusion.3 = f32[24,64,128]{2,1,0:T(8,128)S(1)} fusion(f32[24,64,128]{2,1,0:T(8,128)S(1)} %broadcast.42, s32[256]{0:T(256)S(1)} %get-tuple-element.7, f32[256,64,128]{2,1,0:T(8,128)} %fusion.15), kind=kCustom, calls=%fused_computation.7 | custom fusion | flops 2097152 | bytes 25166848 | tf_op jit(solution)/shard_map/scatter-add | solution.py:50
  399.3 0.8 convert_element_type.45
  400.2 0.6 constant_dynamic-slice_fusion
  400.8 31.7 %all-reduce.11.cloned.1.call-done = bf16[24,64,128]{2,1,0:T(8,128)(2,1)} async-done(((bf16[24,64,128]{2,1,0:T(8,128)(2,1)}), bf16[24,64,128]{2,1,0:T(8,128)(2,1)}) %all-reduce.11.cloned.1.call-update) | async-done | bytes 393232 | tf_op jit(solution)/shard_map/psum | solution.py:53
  432.5 1.2 fusion.6
  433.7 21.4 %psum.63 = f32[64]{0:T(128)S(1)} all-reduce(f32[64]{0:T(128)S(1)} %fusion.6), channel_id=1, replica_groups=mesh['row'=8,'col'=4] {'row'}, use_global_device_ids=true, to_apply=%region_16.17 | all-reduce | flops 64 | bytes 512 | tf_op jit(solution)/shard_map/psum | solution.py:54
  455.1 1.9 fusion.7
  (8 shorter events, 0.1 us)
Async XLA Ops:
  7.2 122.6 %all-reduce.5.cloned.1.call-start = ((), (), s32[]{:S(2)}) async-start(), calls=%async_computation | async-start | bytes 1048576 | tf_op jit(solution)/shard_map/psum | solution.py:41
  54.2 160.2 %all-reduce.7.cloned.1.call-start = ((), (), s32[]{:S(2)}) async-start(), calls=%async_computation.1 | async-start | bytes 786432 | tf_op jit(solution)/shard_map/psum | solution.py:53
  182.0 166.0 %all-reduce.9.cloned.1.call-start = ((), (), s32[]{:S(2)}) async-start(), calls=%async_computation.2 | async-start | bytes 1048576 | tf_op jit(solution)/shard_map/psum | solution.py:41
  278.9 153.7 %all-reduce.11.cloned.1.call-start = ((), (), s32[]{:S(2)}) async-start(), calls=%async_computation.3 | async-start | bytes 786432 | tf_op jit(solution)/shard_map/psum | solution.py:53
Sparse Core Ops, SparseCore 0:
  54.3 75.4 all-reduce.4
  182.1 32.2 all-reduce.6
  279.0 68.9 all-reduce.8
  400.3 32.2 all-reduce.10
where the time goes:
time: 467 us; the launch traced here: 464 us
  waiting for transfers between devices  209 us (45%)
  other arithmetic  124 us (27%)
  blocking collectives  54.2 us (12%)
  matrix products  47.9 us (10%)
  between operations  14.6 us (3%)
  local copies, waits for them, and re-layouts  14.5 us (3%)
    psum x2, waiting for transfers between devices, local(): lax.psum(set_terms.astype(jnp.bfloat16), 'row').astype(jnp.float32)  145 us
    psum x2, waiting for transfers between devices, local(): lax.psum(hub_terms.astype(jnp.bfloat16), 'col').astype(jnp.float32)  64 us
    scatter-add x2, other arithmetic, local(): jax.ops.segment_sum(products, col_slot, num_segments=set_blocks, mode='dr...  52.6 us
    scatter-add x2, other arithmetic, local(): jax.ops.segment_sum(back_products, row_slot, num_segments=slot_count, mod...  52.6 us
    psum x2, blocking collectives, local(): squares = lax.psum(jnp.sum(raw_hub * raw_hub, axis=(0, 2)), 'row')  42.9 us
    dot_general x2, matrix products, local(): jnp.einsum('tkc,trc->tkr', picked_cols, tile_blocks, preferred_element_ty...  27.5 us
    dot_general x2, matrix products, local(): jnp.einsum('tkr,trc->tkc', picked, tile_blocks, preferred_element_type=jn...  20.4 us
    psum x2, blocking collectives, local(): squares = lax.psum(jnp.sum(raw_set * raw_set, axis=(0, 2)), 'col')  11.3 us
  transfers between devices with their start and end apart: 4, of which 4 were waited for; matrix products, arithmetic and copies ran while one was open for 0% of the time, Pallas kernels for 0%

commit v1 on v0

v1 whole, which is shorter than its diff:
```python
import functools

import jax
import jax.numpy as jnp
from jax import lax
from jax.experimental import pallas as pl
from jax.experimental.pallas import tpu as pltpu
from jax.sharding import PartitionSpec as P

ITERS = 2
RB_DEV = 16
MESH = pl.DeviceIdType.MESH
UNROLL = 8
CHUNK = 32


def column_of(row):
    k = row.shape[1]
    eye = lax.broadcasted_iota(jnp.int32, (k, k), 0) == lax.broadcasted_iota(jnp.int32, (k, k), 1)
    return jnp.sum(jnp.where(eye, jnp.broadcast_to(row, (k, k)), 0.0), axis=1, keepdims=True)


def row_of(column, lanes):
    k = column.shape[0]
    eye = lax.broadcasted_iota(jnp.int32, (k, lanes), 0) == lax.broadcasted_iota(jnp.int32, (k, lanes), 1)
    return jnp.sum(jnp.where(eye, jnp.broadcast_to(column, (k, lanes)), 0.0), axis=0, keepdims=True)


def tiles_kernel(transposed, pick_ref, put_ref, x_ref, factor_ref, tiles_ref, out_ref, acc):
    step = pl.program_id(0)
    chunk = tiles_ref.shape[0]
    blocks = out_ref.shape[0]

    @pl.when(step == 0)
    def _():
        acc[...] = jnp.zeros_like(acc)

    dims = (((1,), (1,)), ((), ())) if transposed else (((1,), (0,)), ((), ()))

    @pl.loop(0, chunk // UNROLL)
    def _(i):
        products = []
        for u in range(UNROLL):
            t = i * UNROLL + u
            x = x_ref[pick_ref[step * chunk + t]]
            products.append(lax.dot_general(x, tiles_ref[t], dims, preferred_element_type=jnp.float32))
        for u in range(UNROLL):
            where = put_ref[step * chunk + i * UNROLL + u]
            acc[where] = acc[where] + products[u]

    @pl.when(step == pl.num_programs(0) - 1)
    def _():
        factor = factor_ref[...]

        @pl.loop(0, blocks)
        def _(b):
            out_ref[b] = (acc[b] * factor).astype(jnp.bfloat16)


def tile_sums(transposed, blocks, pick, put, x, factor, tiles):
    slots, side = tiles.shape[0], tiles.shape[1]
    k = x.shape[1]
    chunk = CHUNK
    while slots % chunk:
        chunk //= 2
    grid_spec = pltpu.PrefetchScalarGridSpec(
        num_scalar_prefetch=2,
        grid=(slots // chunk,),
        in_specs=[
            pl.BlockSpec(x.shape, lambda i, *_: (0, 0, 0)),
            pl.BlockSpec(factor.shape, lambda i, *_: (0, 0)),
            pl.BlockSpec((chunk, side, side), lambda i, *_: (i, 0, 0)),
        ],
        out_specs=pl.BlockSpec((blocks, k, side), lambda i, *_: (0, 0, 0)),
        scratch_shapes=[pltpu.VMEM((blocks + 1, k, side), jnp.float32)],
    )
    return pl.pallas_call(
        functools.partial(tiles_kernel, transposed),
        grid_spec=grid_spec,
        out_shape=jax.ShapeDtypeStruct((blocks, k, side), jnp.bfloat16),
        name="hub_tiles" if transposed else "authority_tiles",
    )(pick, put, x, factor, tiles)


def reduce_kernel(
    axis, other, n, m, g, hosts, part_ref, set_ref, factor_ref, own_ref,
    pair_in, hop_out, hop_in, own, sq_axis, sq_other,
    pair_send, pair_recv, hop_send, hop_recv,
    near_send, near_recv, far_send, far_recv,
    sqa_send, sqa_recv, sqo_send, sqo_recv,
):
    me = lax.axis_index(axis)
    mo = lax.axis_index(other)
    lo, hi = me % 2, me // 2
    highs = n // 2
    pair = hi * 2 + (1 - lo)

    def at(index):
        return {axis: index, other: mo}

    barrier = pltpu.get_barrier_semaphore()
    for d in range(1, n):
        pl.semaphore_signal(barrier, inc=1, device_id=at((me + d) % n), device_id_type=MESH)
    for d in range(1, m):
        pl.semaphore_signal(barrier, inc=1, device_id={axis: me, other: (mo + d) % m}, device_id_type=MESH)
    pl.semaphore_wait(barrier, n - 1 + m - 1)

    def group(h, l):
        return pl.ds((h * 2 + l) * g, g)

    def order(d):
        return (hi + 1 + d) % highs

    pair_copies = []
    for d in range(highs):
        h = order(d)
        copy = pltpu.make_async_remote_copy(
            src_ref=part_ref.at[group(h, 1 - lo)], dst_ref=pair_in.at[d],
            send_sem=pair_send.at[d], recv_sem=pair_recv.at[d],
            device_id=at(pair), device_id_type=MESH,
        )
        copy.start()
        pair_copies.append(copy)
    hop_copies = []
    for d in range(highs):
        h = order(d)
        pair_copies[d].wait_recv()
        total = part_ref[group(h, lo)].astype(jnp.float32) + pair_in[d].astype(jnp.float32)
        if d == highs - 1:
            own[...] = total
        else:
            hop_out[d] = total.astype(jnp.bfloat16)
            copy = pltpu.make_async_remote_copy(
                src_ref=hop_out.at[d], dst_ref=hop_in.at[d],
                send_sem=hop_send.at[d], recv_sem=hop_recv.at[d],
                device_id=at(h * 2 + lo), device_id_type=MESH,
            )
            copy.start()
            hop_copies.append(copy)
    for copy in hop_copies:
        copy.wait_recv()
    total = own[...]
    for d in range(highs - 1):
        total = total + hop_in[d].astype(jnp.float32)
    own[...] = total
    set_ref[group(hi, lo)] = total.astype(jnp.bfloat16)
    squares = jnp.sum(total * total, axis=0)
    sq_axis[me] = jnp.broadcast_to(row_of(jnp.sum(squares, axis=1, keepdims=True), 128), (8, 128))

    sqa_copies = []
    for d in range(1, n):
        copy = pltpu.make_async_remote_copy(
            src_ref=sq_axis.at[me], dst_ref=sq_axis.at[me],
            send_sem=sqa_send.at[d - 1], recv_sem=sqa_recv.at[d - 1],
            device_id=at((me + d) % n), device_id_type=MESH,
        )
        copy.start()
        sqa_copies.append(copy)
    far_copies = []
    for d in range(highs - 1):
        copy = pltpu.make_async_remote_copy(
            src_ref=set_ref.at[group(hi, lo)], dst_ref=set_ref.at[group(hi, lo)],
            send_sem=far_send.at[d], recv_sem=far_recv.at[d],
            device_id=at(order(d) * 2 + lo), device_id_type=MESH,
        )
        copy.start()
        far_copies.append(copy)

    def to_partner(d, h):
        copy = pltpu.make_async_remote_copy(
            src_ref=set_ref.at[group(h, lo)], dst_ref=set_ref.at[group(h, lo)],
            send_sem=near_send.at[d], recv_sem=near_recv.at[d],
            device_id=at(pair), device_id_type=MESH,
        )
        copy.start()
        return copy

    near_copies = [to_partner(highs - 1, hi)]

    for copy in sqa_copies:
        copy.wait_recv()
    sq_other[mo] = jnp.sum(sq_axis[...], axis=0)
    sqo_copies = []
    for d in range(1, m):
        copy = pltpu.make_async_remote_copy(
            src_ref=sq_other.at[mo], dst_ref=sq_other.at[mo],
            send_sem=sqo_send.at[d - 1], recv_sem=sqo_recv.at[d - 1],
            device_id={axis: me, other: (mo + d) % m}, device_id_type=MESH,
        )
        copy.start()
        sqo_copies.append(copy)

    for d in range(highs - 1):
        far_copies[d].wait_recv()
        near_copies.append(to_partner(d, (hi + highs - 1 - d) % highs))
    for copy in sqo_copies:
        copy.wait_recv()
    all_squares = jnp.sum(sq_other[...], axis=0)
    factor_row = 1.0 / jnp.sqrt(all_squares / hosts + 1.0)
    k = factor_ref.shape[0]
    factor = jnp.broadcast_to(column_of(factor_row[0:1, :k]), factor_ref.shape)
    factor_ref[...] = factor
    own_ref[...] = (own[...] * factor[None]).astype(jnp.bfloat16)
    for copy in near_copies:
        copy.wait_recv()
    for copy in pair_copies + hop_copies + sqa_copies + far_copies + near_copies + sqo_copies:
        copy.wait_send()


def reduce_set(axis, other, n, m, hosts, collective_id, part):
    blocks, k, side = part.shape
    g = blocks // n
    highs = n // 2
    vmem = pl.BlockSpec(memory_space=pltpu.VMEM)
    dma = lambda count: pltpu.SemaphoreType.DMA((max(count, 1),))
    return pl.pallas_call(
        functools.partial(reduce_kernel, axis, other, n, m, g, hosts),
        out_shape=(
            jax.ShapeDtypeStruct((blocks, k, side), jnp.bfloat16),
            jax.ShapeDtypeStruct((k, side), jnp.float32),
            jax.ShapeDtypeStruct((g, k, side), jnp.bfloat16),
        ),
        in_specs=[vmem],
        out_specs=(vmem, vmem, vmem),
        scratch_shapes=[
            pltpu.VMEM((highs, g, k, side), jnp.bfloat16),
            pltpu.VMEM((max(highs - 1, 1), g, k, side), jnp.bfloat16),
            pltpu.VMEM((max(highs - 1, 1), g, k, side), jnp.bfloat16),
            pltpu.VMEM((g, k, side), jnp.float32),
            pltpu.VMEM((n, 8, 128), jnp.float32),
            pltpu.VMEM((m, 8, 128), jnp.float32),
            dma(highs), dma(highs), dma(highs - 1), dma(highs - 1),
            dma(highs), dma(highs), dma(highs - 1), dma(highs - 1),
            dma(n - 1), dma(n - 1), dma(m - 1), dma(m - 1),
        ],
        compiler_params=pltpu.CompilerParams(collective_id=collective_id, has_side_effects=True),
        name="reduce_" + axis,
    )(part)


def local(row_devs, col_devs, hub_seeds, tile_blocks, tile_rows, tile_cols, tile_count, row_blocks):
    own_row = lax.axis_index("row")
    slot_count, k = hub_seeds.shape[0], hub_seeds.shape[1]
    tile_slots, tile_side = tile_blocks.shape[0], tile_blocks.shape[1]
    group_len = RB_DEV // col_devs
    set_blocks = group_len * row_devs
    host_count = RB_DEV * row_devs * tile_side
    before = jnp.arange(row_devs, dtype=jnp.int32) < own_row
    first_block = jnp.sum(jnp.where(before, row_blocks, 0))
    live = jnp.arange(tile_slots, dtype=jnp.int32) < tile_count[0]
    row_slot = tile_rows - first_block
    col_slot = tile_cols // group_len // col_devs * group_len + tile_cols % group_len
    row_pick = jnp.where(live, row_slot, 0)
    col_pick = jnp.where(live, col_slot, 0)
    row_put = jnp.where(live, row_slot, slot_count)
    col_put = jnp.where(live, col_slot, set_blocks)
    hub = hub_seeds
    factor = jnp.ones((k, tile_side), jnp.float32)
    for iteration in range(ITERS):
        part = tile_sums(False, set_blocks, row_pick, col_put, hub, factor, tile_blocks)
        column_set, factor, authority = reduce_set("row", "col", row_devs, col_devs, host_count, 0, part)
        part = tile_sums(True, slot_count, col_pick, row_put, column_set, factor, tile_blocks)
        hub, factor, _ = reduce_set("col", "row", col_devs, row_devs, host_count, 1, part)
    hub_scores = (hub.astype(jnp.float32) * factor[None]).astype(jnp.bfloat16)
    return (authority, hub_scores)


def solution(mesh):
    return jax.shard_map(
        functools.partial(local, mesh.shape["row"], mesh.shape["col"]),
        mesh=mesh,
        in_specs=(
            P("row", None, None),
            P(("row", "col"), None, None),
            P(("row", "col")),
            P(("row", "col")),
            P(("row", "col")),
            P(),
        ),
        out_specs=(P(("row", "col"), None, None), P("row", None, None)),
        check_vma=False,
    )
```

time: 467 us -> 145 us (0.31)
  waiting for transfers between devices: 209 us -> 0 us
  Pallas kernels: 0 us -> 135 us
  other arithmetic: 124 us -> 5.67 us
  blocking collectives: 54.2 us -> 0 us
  matrix products: 47.9 us -> 0 us
  between operations: 14.6 us -> 1.32 us
  local copies, waits for them, and re-layouts: 14.5 us -> 1.25 us
    psum x4 -> x0, waiting for transfers between devices: 209 us -> none  [the longest x2 145 us: local(): lax.psum(set_terms.astype(jnp.bfloat16), 'row').astype(jnp.float32)]
    pallas_call x0 -> x8, Pallas kernels: none -> 135 us  [the longest x4 87.4 us: reduce_set(): pl.pallas_call(functools.partial(reduce_kernel, axis, other, n, m, g, hos...]
    scatter-add x4 -> x0, other arithmetic: 105 us -> none  [the longest x2 52.6 us: local(): jax.ops.segment_sum(products, col_slot, num_segments=set_blocks, mode='dr...]
    psum x4 -> x0, blocking collectives: 54.2 us -> none  [the longest x2 42.9 us: local(): squares = lax.psum(jnp.sum(raw_hub * raw_hub, axis=(0, 2)), 'row')]
    dot_general x4 -> x0, matrix products: 47.9 us -> none  [the longest x2 27.5 us: local(): jnp.einsum('tkc,trc->tkr', picked_cols, tile_blocks, preferred_element_ty...]
    gather x4 -> x0, local copies, waits for them, and re-layouts: 12.3 us -> none  [the longest x2 6.14 us: local(): picked_cols = jnp.take(column_set, col_pick, axis=0, mode='clip')]
    convert_element_type x8 -> x1, other arithmetic: 9.01 us -> 1.85 us  [local(): hub_scores = (hub.astype(jnp.float32) * factor[None]).astype(jnp.bfloat16)]
    reduce_sum x4 -> x0, other arithmetic: 4.87 us -> none  [the longest x2 2.51 us: local(): squares = lax.psum(jnp.sum(raw_set * raw_set, axis=(0, 2)), 'col')]
  transfers between devices with their start and end apart: 4 -> 0, of which waited for: 4 -> 0; matrix products, arithmetic and copies ran while one was open for 0% -> 0% of each run, Pallas kernels for 0% -> 0%
where the time goes in v1:
time: 145 us; the launch traced here: 143 us
  Pallas kernels  135 us (93%)
  other arithmetic  5.67 us (4%)
    pallas_call x4, Pallas kernels, reduce_set(): pl.pallas_call(functools.partial(reduce_kernel, axis, other, n, m, g, hos...  87.4 us
    pallas_call x4, Pallas kernels, tile_sums(): pl.pallas_call(functools.partial(tiles_kernel, transposed), grid_spec=gri...  47.7 us

profile of v1, /device:TPU:0, one launch (start us, length us, event | category | flops | bytes accessed | tf_op | source)
XLA Modules:
  0.0 143.4 jit_solution(4019537752117684143)
XLA Ops:
  1.3 1.3 fusion.5
  2.6 1.9 %fusion.1 = (s32[256]{0:T(256)}, s32[256]{0:T(256)}, s32[256]{0:T(256)}, s32[256]{0:T(256)S(1)}) fusion(s32[256]{0:T(256)} %param.8, s32[]{:T(128)} %fusion.5, s32[]{:T(128)} %bitcast.1, s32[256]{0:T(256)} %param.9), kind=kLoop, calls=%fused_computation.13 | loop fusion | flops 10496 | bytes 6152 | tf_op jit(solution)/shard_map/jit(_where)/select_n | solution.py:255
  4.5 0.6 fusion.3.put_ref
  5.1 0.6 broadcast_in_dim.23.factor_ref
  5.7 11.3 %authority_tiles.2.part_ref = bf16[32,64,128]{2,1,0:T(8,128)(2,1)} custom-call(s32[256]{0:T(256)} %get-tuple-element.23.pick_ref, s32[256]{0:T(256)} %fusion.3.put_ref, bf16[24,64,128]{2,1,0:T(8,128)(2,1)} %x_ref.1, f32[64,128]{1,0:T(8,128)} %broadcast_in_dim.23.factor_ref, bf16[256,128,128]{2,1,0:T(8,128)(2,1)} %tiles_ref.7), custom_call_target="tpu_custom_call" | custom-call | tf_op jit(solution)/shard_map/authority_tiles/pallas_call | solution.py:77
  17.0 28.3 %reduce_row.2 = (bf16[32,64,128]{2,1,0:T(8,128)(2,1)}, f32[64,128]{1,0:T(8,128)}, bf16[4,64,128]{2,1,0:T(8,128)(2,1)}) custom-call(bf16[32,64,128]{2,1,0:T(8,128)(2,1)} %authority_tiles.2.part_ref), custom_call_target="tpu_custom_call" | custom-call | tf_op jit(solution)/shard_map/reduce_row/pallas_call | solution.py:216
  45.3 12.5 %hub_tiles.2.part_ref = bf16[24,64,128]{2,1,0:T(8,128)(2,1)} custom-call(s32[256]{0:T(256)} %get-tuple-element.24.pick_ref, s32[256]{0:T(256)} %get-tuple-element.22.put_ref, bf16[32,64,128]{2,1,0:T(8,128)(2,1)} %get-tuple-element.11.x_ref, f32[64,128]{1,0:T(8,128)} %get-tuple-element.12.factor_ref, bf16[256,128,128]{2,1,0:T(8,128)(2,1)} %tiles_ref.7), custom_call_target="tpu_custom_call" | custom-call | tf_op jit(solution)/shard_map/hub_tiles/pallas_call | solution.py:77
  57.9 16.6 %reduce_col.2 = (bf16[24,64,128]{2,1,0:T(8,128)(2,1)}, f32[64,128]{1,0:T(8,128)}, bf16[6,64,128]{2,1,0:T(8,128)(2,1)}) custom-call(bf16[24,64,128]{2,1,0:T(8,128)(2,1)} %hub_tiles.2.part_ref), custom_call_target="tpu_custom_call" | custom-call | tf_op jit(solution)/shard_map/reduce_col/pallas_call | solution.py:216
  74.5 11.3 %authority_tiles.3.part_ref = bf16[32,64,128]{2,1,0:T(8,128)(2,1)} custom-call(s32[256]{0:T(256)} %get-tuple-element.23.pick_ref, s32[256]{0:T(256)} %fusion.3.put_ref, bf16[24,64,128]{2,1,0:T(8,128)(2,1)} %get-tuple-element.13.x_ref, f32[64,128]{1,0:T(8,128)} %get-tuple-element.14.factor_ref, bf16[256,128,128]{2,1,0:T(8,128)(2,1)} %tiles_ref.7), custom_call_target="tpu_custom_call" | custom-call | tf_op jit(solution)/shard_map/authority_tiles/pallas_call | solution.py:77
  85.7 25.3 %reduce_row.3 = (bf16[32,64,128]{2,1,0:T(8,128)(2,1)}, f32[64,128]{1,0:T(8,128)}, bf16[4,64,128]{2,1,0:T(8,128)(2,1)}) custom-call(bf16[32,64,128]{2,1,0:T(8,128)(2,1)} %authority_tiles.3.part_ref), custom_call_target="tpu_custom_call" | custom-call | tf_op jit(solution)/shard_map/reduce_row/pallas_call | solution.py:216
  111.0 0.0 copy-start
  111.1 12.7 %hub_tiles.3.part_ref = bf16[24,64,128]{2,1,0:T(8,128)(2,1)} custom-call(s32[256]{0:T(256)} %get-tuple-element.24.pick_ref, s32[256]{0:T(256)} %get-tuple-element.22.put_ref, bf16[32,64,128]{2,1,0:T(8,128)(2,1)} %get-tuple-element.16.x_ref, f32[64,128]{1,0:T(8,128)} %get-tuple-element.17.factor_ref, bf16[256,128,128]{2,1,0:T(8,128)(2,1)} %tiles_ref.7), custom_call_target="tpu_custom_call" | custom-call | tf_op jit(solution)/shard_map/hub_tiles/pallas_call | solution.py:77
  123.7 17.2 %reduce_col.3 = (bf16[24,64,128]{2,1,0:T(8,128)(2,1)}, f32[64,128]{1,0:T(8,128)}, bf16[6,64,128]{2,1,0:T(8,128)(2,1)}) custom-call(bf16[24,64,128]{2,1,0:T(8,128)(2,1)} %hub_tiles.3.part_ref), custom_call_target="tpu_custom_call" | custom-call | tf_op jit(solution)/shard_map/reduce_col/pallas_call | solution.py:216
  140.9 1.8 %multiply_convert_fusion = bf16[24,64,128]{2,1,0:T(8,128)(2,1)} fusion(bf16[24,64,128]{2,1,0:T(8,128)(2,1)} %get-tuple-element.18, f32[64,128]{1,0:T(8,128)} %get-tuple-element.19), kind=kLoop, calls=%fused_computation | loop fusion | flops 589824 | bytes 819200 | tf_op jit(solution)/shard_map/convert_element_type | solution.py:264
  142.8 0.0 copy-done
  142.8 0.6 copy.10
Async XLA Ops:
  111.0 31.7 %copy-start = (bf16[4,64,128]{2,1,0:T(8,128)(2,1)S(1)}, bf16[4,64,128]{2,1,0:T(8,128)(2,1)}, u32[]{:S(2)}) copy-start(bf16[4,64,128]{2,1,0:T(8,128)(2,1)} %get-tuple-element.28) | copy-start | bytes 196612

commit v2 on v1

v2 whole, which is shorter than its diff:
```python
import functools

import jax
import jax.numpy as jnp
from jax import lax
from jax.experimental import pallas as pl
from jax.experimental.pallas import tpu as pltpu
from jax.sharding import PartitionSpec as P

ITERS = 2
RB_DEV = 16
MESH = pl.DeviceIdType.MESH
UNROLL = 64
CHUNK = 64


def column_of(row):
    k = row.shape[1]
    eye = lax.broadcasted_iota(jnp.int32, (k, k), 0) == lax.broadcasted_iota(jnp.int32, (k, k), 1)
    return jnp.sum(jnp.where(eye, jnp.broadcast_to(row, (k, k)), 0.0), axis=1, keepdims=True)


def row_of(column, lanes):
    k = column.shape[0]
    eye = lax.broadcasted_iota(jnp.int32, (k, lanes), 0) == lax.broadcasted_iota(jnp.int32, (k, lanes), 1)
    return jnp.sum(jnp.where(eye, jnp.broadcast_to(column, (k, lanes)), 0.0), axis=0, keepdims=True)


def tiles_kernel(transposed, pick_ref, put_ref, x_ref, tiles_ref, out_ref, acc):
    step = pl.program_id(0)
    chunk = tiles_ref.shape[0]
    blocks = out_ref.shape[0]

    @pl.when(step == 0)
    def _():
        acc[...] = jnp.zeros_like(acc)

    dims = (((1,), (1,)), ((), ())) if transposed else (((1,), (0,)), ((), ()))

    side = tiles_ref.shape[1]
    k = x_ref.shape[1]

    @pl.loop(0, chunk // UNROLL)
    def _(i):
        products = []
        for u in range(0, UNROLL, 2):
            t = i * UNROLL + u
            x = jnp.concatenate([x_ref[pick_ref[step * chunk + t + v]] for v in range(2)], axis=0)
            if transposed:
                both = tiles_ref[pl.ds(t, 2)].reshape(2 * side, side)
            else:
                both = jnp.concatenate([tiles_ref[t], tiles_ref[t + 1]], axis=1)
            product = lax.dot_general(x, both, dims, preferred_element_type=jnp.float32)
            products += [product[:k, :side], product[k:, side:]]
        for u in range(UNROLL):
            where = put_ref[step * chunk + i * UNROLL + u]
            acc[where] = acc[where] + products[u]

    @pl.when(step == pl.num_programs(0) - 1)
    def _():
        @pl.loop(0, blocks)
        def _(b):
            out_ref[b] = acc[b].astype(jnp.bfloat16)


def tile_sums(transposed, blocks, pick, put, x, tiles):
    slots, side = tiles.shape[0], tiles.shape[1]
    k = x.shape[1]
    chunk = CHUNK
    while slots % chunk:
        chunk //= 2
    grid_spec = pltpu.PrefetchScalarGridSpec(
        num_scalar_prefetch=2,
        grid=(slots // chunk,),
        in_specs=[
            pl.BlockSpec(x.shape, lambda i, *_: (0, 0, 0)),
            pl.BlockSpec((chunk, side, side), lambda i, *_: (i, 0, 0)),
        ],
        out_specs=pl.BlockSpec((blocks, k, side), lambda i, *_: (0, 0, 0)),
        scratch_shapes=[pltpu.VMEM((blocks + 1, k, side), jnp.float32)],
    )
    return pl.pallas_call(
        functools.partial(tiles_kernel, transposed),
        grid_spec=grid_spec,
        out_shape=jax.ShapeDtypeStruct((blocks, k, side), jnp.bfloat16),
        name="hub_tiles" if transposed else "authority_tiles",
    )(pick, put, x, tiles)


def factor_of(squares, hosts, k, side):
    row = 1.0 / jnp.sqrt(squares / hosts + 1.0)
    return jnp.broadcast_to(column_of(row[0:1, :k]), (k, side))


def reduce_kernel(axis, other, n, m, g, hosts, scaled, final, *refs):
    refs = list(refs)
    part_ref = refs.pop(0)
    sq_ref = refs.pop(0) if scaled else None
    set_ref = refs.pop(0)
    if final:
        before_ref, after_ref = refs.pop(0), refs.pop(0)
    else:
        sq_out_ref, own = refs.pop(0), refs.pop(0)
    pair_in, hop_out, hop_in, sq_before, sq_axis, sq_other = refs[:6]
    refs = refs[6:]
    if final:
        own = refs.pop(0)
    (pair_send, pair_recv, hop_send, hop_recv, near_send, near_recv, far_send, far_recv,
     sqb_send, sqb_recv, sqa_send, sqa_recv, sqo_send, sqo_recv) = refs
    k, side = part_ref.shape[1], part_ref.shape[2]
    me = lax.axis_index(axis)
    mo = lax.axis_index(other)
    lo, hi = me % 2, me // 2
    highs = n // 2
    pair = hi * 2 + (1 - lo)
    waits = []

    def at(index):
        return {axis: index, other: mo}

    def send(src, dst, send_sem, recv_sem, device):
        copy = pltpu.make_async_remote_copy(
            src_ref=src, dst_ref=dst, send_sem=send_sem, recv_sem=recv_sem,
            device_id=device, device_id_type=MESH,
        )
        copy.start()
        waits.append(copy)
        return copy

    barrier = pltpu.get_barrier_semaphore()
    for d in range(1, n):
        pl.semaphore_signal(barrier, inc=1, device_id=at((me + d) % n), device_id_type=MESH)
    if final:
        for d in range(1, m):
            pl.semaphore_signal(barrier, inc=1, device_id={axis: me, other: (mo + d) % m}, device_id_type=MESH)
    pl.semaphore_wait(barrier, n - 1 + (m - 1 if final else 0))

    def group(h, l):
        return pl.ds((h * 2 + l) * g, g)

    def order(d):
        return (hi + 1 + d) % highs

    pair_copies = [
        send(part_ref.at[group(order(d), 1 - lo)], pair_in.at[d], pair_send.at[d], pair_recv.at[d], at(pair))
        for d in range(highs)
    ]
    sqb_copies = []
    if scaled:
        sq_before[me] = sq_ref[...]
        sqb_copies = [
            send(sq_ref, sq_before.at[me], sqb_send.at[d - 1], sqb_recv.at[d - 1], at((me + d) % n))
            for d in range(1, n)
        ]
    hop_copies = []
    for d in range(highs):
        h = order(d)
        pair_copies[d].wait_recv()
        total = part_ref[group(h, lo)].astype(jnp.float32) + pair_in[d].astype(jnp.float32)
        if d == highs - 1:
            own[...] = total
        else:
            hop_out[d] = total.astype(jnp.bfloat16)
            hop_copies.append(send(hop_out.at[d], hop_in.at[d], hop_send.at[d], hop_recv.at[d], at(h * 2 + lo)))
    if scaled:
        for copy in sqb_copies:
            copy.wait_recv()
        factor = factor_of(jnp.sum(sq_before[...], axis=0), hosts, k, side)
        if final:
            before_ref[...] = factor
    for copy in hop_copies:
        copy.wait_recv()
    total = own[...]
    for d in range(highs - 1):
        total = total + hop_in[d].astype(jnp.float32)
    if scaled:
        total = total * factor[None]
    own[...] = total
    set_ref[group(hi, lo)] = total.astype(jnp.bfloat16)

    far_copies = [
        send(set_ref.at[group(hi, lo)], set_ref.at[group(hi, lo)], far_send.at[d], far_recv.at[d], at(order(d) * 2 + lo))
        for d in range(highs - 1)
    ]

    def to_partner(d, h):
        return send(set_ref.at[group(h, lo)], set_ref.at[group(h, lo)], near_send.at[d], near_recv.at[d], at(pair))

    near_copies = [to_partner(highs - 1, hi)]
    squares = jnp.sum(total * total, axis=0)
    sq_axis[me] = jnp.broadcast_to(row_of(jnp.sum(squares, axis=1, keepdims=True), 128), (8, 128))
    sqa_copies = [
        send(sq_axis.at[me], sq_axis.at[me], sqa_send.at[d - 1], sqa_recv.at[d - 1], at((me + d) % n))
        for d in range(1, n)
    ]

    def axis_squares():
        for copy in sqa_copies:
            copy.wait_recv()
        return jnp.sum(sq_axis[...], axis=0)

    sqo_copies = []
    if final:
        sq_other[mo] = axis_squares()
        sqo_copies = [
            send(sq_other.at[mo], sq_other.at[mo], sqo_send.at[d - 1], sqo_recv.at[d - 1], {axis: me, other: (mo + d) % m})
            for d in range(1, m)
        ]
    for d in range(highs - 1):
        far_copies[d].wait_recv()
        near_copies.append(to_partner(d, (hi + highs - 1 - d) % highs))
    if final:
        for copy in sqo_copies:
            copy.wait_recv()
        after_ref[...] = factor_of(jnp.sum(sq_other[...], axis=0), hosts, k, side)
    else:
        sq_out_ref[...] = axis_squares()
    for copy in near_copies:
        copy.wait_recv()
    for copy in waits:
        copy.wait_send()


def reduce_set(axis, other, n, m, hosts, collective_id, final, part, squares=None):
    blocks, k, side = part.shape
    g = blocks // n
    highs = n // 2
    vmem = pl.BlockSpec(memory_space=pltpu.VMEM)
    dma = lambda count: pltpu.SemaphoreType.DMA((max(count, 1),))
    scaled = squares is not None
    table = jax.ShapeDtypeStruct((k, side), jnp.float32)
    outs = [jax.ShapeDtypeStruct((blocks, k, side), jnp.bfloat16)]
    scratch = []
    if final:
        outs += [table, table]
        scratch = [pltpu.VMEM((g, k, side), jnp.float32)]
    else:
        outs += [jax.ShapeDtypeStruct((8, 128), jnp.float32), jax.ShapeDtypeStruct((g, k, side), jnp.float32)]
    operands = (part, squares) if scaled else (part,)
    return pl.pallas_call(
        functools.partial(reduce_kernel, axis, other, n, m, g, hosts, scaled, final),
        out_shape=tuple(outs),
        in_specs=[vmem] * len(operands),
        out_specs=(vmem,) * len(outs),
        scratch_shapes=[
            pltpu.VMEM((highs, g, k, side), jnp.bfloat16),
            pltpu.VMEM((max(highs - 1, 1), g, k, side), jnp.bfloat16),
            pltpu.VMEM((max(highs - 1, 1), g, k, side), jnp.bfloat16),
            pltpu.VMEM((n, 8, 128), jnp.float32),
            pltpu.VMEM((n, 8, 128), jnp.float32),
            pltpu.VMEM((m, 8, 128), jnp.float32),
            *scratch,
            dma(highs), dma(highs), dma(highs - 1), dma(highs - 1),
            dma(highs), dma(highs), dma(highs - 1), dma(highs - 1),
            dma(n - 1), dma(n - 1), dma(n - 1), dma(n - 1), dma(m - 1), dma(m - 1),
        ],
        compiler_params=pltpu.CompilerParams(collective_id=collective_id, has_side_effects=True),
        name="reduce_" + axis,
    )(*operands)


def local(row_devs, col_devs, hub_seeds, tile_blocks, tile_rows, tile_cols, tile_count, row_blocks):
    own_row = lax.axis_index("row")
    slot_count = hub_seeds.shape[0]
    tile_slots, tile_side = tile_blocks.shape[0], tile_blocks.shape[1]
    group_len = RB_DEV // col_devs
    set_blocks = group_len * row_devs
    host_count = RB_DEV * row_devs * tile_side
    first_block = jnp.zeros((1,), jnp.int32)
    for r in range(row_devs - 1):
        first_block = first_block + jnp.where(own_row > r, row_blocks[r:r + 1], 0)
    live = jnp.arange(tile_slots, dtype=jnp.int32) < tile_count
    row_slot = tile_rows - first_block
    col_slot = tile_cols // group_len // col_devs * group_len + tile_cols % group_len
    row_pick = jnp.where(live, row_slot, 0)
    col_pick = jnp.where(live, col_slot, 0)
    row_put = jnp.where(live, row_slot, slot_count)
    col_put = jnp.where(live, col_slot, set_blocks)
    hub, squares = hub_seeds, None
    for iteration in range(ITERS):
        last = iteration == ITERS - 1
        part = tile_sums(False, set_blocks, row_pick, col_put, hub, tile_blocks)
        column_set, squares, own = reduce_set(
            "row", "col", row_devs, col_devs, host_count, iteration, False, part, squares)
        part = tile_sums(True, slot_count, col_pick, row_put, column_set, tile_blocks)
        hub, squares, rest = reduce_set(
            "col", "row", col_devs, row_devs, host_count, ITERS + iteration, last, part, squares)
    authority = (own * squares[None]).astype(jnp.bfloat16)
    hub_scores = (hub.astype(jnp.float32) * rest[None]).astype(jnp.bfloat16)
    return (authority, hub_scores)


def solution(mesh):
    return jax.shard_map(
        functools.partial(local, mesh.shape["row"], mesh.shape["col"]),
        mesh=mesh,
        in_specs=(
            P("row", None, None),
            P(("row", "col"), None, None),
            P(("row", "col")),
            P(("row", "col")),
            P(("row", "col")),
            P(),
        ),
        out_specs=(P(("row", "col"), None, None), P("row", None, None)),
        check_vma=False,
    )
```

time: 145 us -> 128 us (0.88)
  Pallas kernels: 135 us -> 115 us
  between operations: 1.32 us -> 5.75 us
    pallas_call x4, Pallas kernels: 47.7 us -> 29.4 us  [tile_sums(): pl.pallas_call(functools.partial(tiles_kernel, transposed), grid_spec=gri...]
    slice x0 -> x1, local copies, waits for them, and re-layouts: none -> 1.59 us  [local(): first_block = first_block + jnp.where(own_row > r, row_blocks[r:r + 1], 0)]
    pallas_call x4, Pallas kernels: 87.4 us -> 85.9 us  [reduce_set(): pl.pallas_call(functools.partial(reduce_kernel, axis, other, n, m, g, hos...]
    convert_element_type x1 -> x2, other arithmetic: 1.85 us -> 3.25 us  [the longest x1 1.84 us: local(): hub_scores = (hub.astype(jnp.float32) * rest[None]).astype(jnp.bfloat16)]
where the time goes in v2:
time: 128 us
  Pallas kernels  115 us (90%)
  between operations  5.75 us (4%)
  other arithmetic  5.11 us (4%)
  local copies, waits for them, and re-layouts  1.6 us (1%)
    pallas_call x4, Pallas kernels, reduce_set(): pl.pallas_call(functools.partial(reduce_kernel, axis, other, n, m, g, hos...  85.9 us
    pallas_call x4, Pallas kernels, tile_sums(): pl.pallas_call(functools.partial(tiles_kernel, transposed), grid_spec=gri...  29.4 us

profile of v2, /device:TPU:0, one launch (start us, length us, event | category | flops | bytes accessed | tf_op | source)
XLA Modules:
  0.0 127.8 jit_solution(10309453409436197997)
XLA Ops:
  1.3 1.6 %fusion.6 = (s32[1]{0:T(128)}, s32[1]{0:T(128)}, s32[1]{0:T(128)}, s32[1]{0:T(128)}, s32[1]{0:T(128)}, /*index=5*/s32[1]{0:T(128)}, s32[1]{0:T(128)}) fusion(s32[8]{0:T(128)} %param.11), kind=kLoop, calls=%fused_computation.17 | loop fusion | bytes 56 | tf_op jit(solution)/shard_map/slice | solution.py:271
  7.3 1.3 %fusion.1 = (s32[256]{0:T(256)}, s32[256]{0:T(256)}, s32[256]{0:T(256)}, s32[256]{0:T(256)S(1)}) fusion(s32[256]{0:T(256)} %param.8, s32[]{:T(128)} %bitcast.8, s32[]{:T(128)} %bitcast.9, s32[256]{0:T(256)} %param.9), kind=kLoop, calls=%fused_computation.13 | loop fusion | flops 10496 | bytes 6152 | tf_op jit(solution)/shard_map/jit(_where)/select_n | solution.py:277
  8.6 0.6 fusion.3.put_ref
  9.2 7.3 %authority_tiles.2.refs_0_ = bf16[32,64,128]{2,1,0:T(8,128)(2,1)} custom-call(s32[256]{0:T(256)} %get-tuple-element.25.pick_ref, s32[256]{0:T(256)} %fusion.3.put_ref, bf16[24,64,128]{2,1,0:T(8,128)(2,1)} %x_ref.1, bf16[256,128,128]{2,1,0:T(8,128)(2,1)} %tiles_ref.7), custom_call_target="tpu_custom_call" | custom-call | tf_op jit(solution)/shard_map/authority_tiles/pallas_call | solution.py:82
  16.5 28.0 %reduce_row.2 = (bf16[32,64,128]{2,1,0:T(8,128)(2,1)}, f32[8,128]{1,0:T(8,128)}, f32[4,64,128]{2,1,0:T(8,128)}) custom-call(bf16[32,64,128]{2,1,0:T(8,128)(2,1)} %authority_tiles.2.refs_0_), custom_call_target="tpu_custom_call" | custom-call | tf_op jit(solution)/shard_map/reduce_row/pallas_call | solution.py:240
  44.5 7.3 %hub_tiles.2.refs_0_ = bf16[24,64,128]{2,1,0:T(8,128)(2,1)} custom-call(s32[256]{0:T(256)} %get-tuple-element.33.pick_ref, s32[256]{0:T(256)} %get-tuple-element.24.put_ref, bf16[32,64,128]{2,1,0:T(8,128)(2,1)} %get-tuple-element.12.x_ref, bf16[256,128,128]{2,1,0:T(8,128)(2,1)} %tiles_ref.7), custom_call_target="tpu_custom_call" | custom-call | tf_op jit(solution)/shard_map/hub_tiles/pallas_call | solution.py:82
  51.8 14.0 %reduce_col.2 = (bf16[24,64,128]{2,1,0:T(8,128)(2,1)}, f32[8,128]{1,0:T(8,128)}, f32[6,64,128]{2,1,0:T(8,128)}) custom-call(bf16[24,64,128]{2,1,0:T(8,128)(2,1)} %hub_tiles.2.refs_0_, f32[8,128]{1,0:T(8,128)} %get-tuple-element.13.refs_1_), custom_call_target="tpu_custom_call" | custom-call | tf_op jit(solution)/shard_map/reduce_col/pallas_call | solution.py:240
  65.8 7.3 %authority_tiles.3.refs_0_ = bf16[32,64,128]{2,1,0:T(8,128)(2,1)} custom-call(s32[256]{0:T(256)} %get-tuple-element.25.pick_ref, s32[256]{0:T(256)} %fusion.3.put_ref, bf16[24,64,128]{2,1,0:T(8,128)(2,1)} %get-tuple-element.14.x_ref, bf16[256,128,128]{2,1,0:T(8,128)(2,1)} %tiles_ref.7), custom_call_target="tpu_custom_call" | custom-call | tf_op jit(solution)/shard_map/authority_tiles/pallas_call | solution.py:82
  73.2 25.1 %reduce_row.3 = (bf16[32,64,128]{2,1,0:T(8,128)(2,1)}, f32[8,128]{1,0:T(8,128)}, f32[4,64,128]{2,1,0:T(8,128)}) custom-call(bf16[32,64,128]{2,1,0:T(8,128)(2,1)} %authority_tiles.3.refs_0_, f32[8,128]{1,0:T(8,128)} %get-tuple-element.15.refs_1_), custom_call_target="tpu_custom_call" | custom-call | tf_op jit(solution)/shard_map/reduce_row/pallas_call | solution.py:240
  98.3 0.0 copy-start
  98.3 7.4 %hub_tiles.3.refs_0_ = bf16[24,64,128]{2,1,0:T(8,128)(2,1)} custom-call(s32[256]{0:T(256)} %get-tuple-element.33.pick_ref, s32[256]{0:T(256)} %get-tuple-element.24.put_ref, bf16[32,64,128]{2,1,0:T(8,128)(2,1)} %get-tuple-element.17.x_ref, bf16[256,128,128]{2,1,0:T(8,128)(2,1)} %tiles_ref.7), custom_call_target="tpu_custom_call" | custom-call | tf_op jit(solution)/shard_map/hub_tiles/pallas_call | solution.py:82
  105.8 18.7 %reduce_col.3 = (bf16[24,64,128]{2,1,0:T(8,128)(2,1)}, f32[64,128]{1,0:T(8,128)}, f32[64,128]{1,0:T(8,128)}) custom-call(bf16[24,64,128]{2,1,0:T(8,128)(2,1)} %hub_tiles.3.refs_0_, f32[8,128]{1,0:T(8,128)} %get-tuple-element.18.refs_1_), custom_call_target="tpu_custom_call" | custom-call | tf_op jit(solution)/shard_map/reduce_col/pallas_call | solution.py:240
  124.5 0.0 copy-done
  124.5 1.4 %multiply_convert_fusion.1 = bf16[4,64,128]{2,1,0:T(8,128)(2,1)} fusion(f32[4,64,128]{2,1,0:T(8,128)S(1)} %copy-done, f32[64,128]{1,0:T(8,128)} %get-tuple-element.19), kind=kLoop, calls=%fused_computation.1 | loop fusion | flops 65536 | bytes 229376 | tf_op jit(solution)/shard_map/convert_element_type | solution.py:288
  125.9 1.8 %multiply_convert_fusion = bf16[24,64,128]{2,1,0:T(8,128)(2,1)} fusion(bf16[24,64,128]{2,1,0:T(8,128)(2,1)} %get-tuple-element.20, f32[64,128]{1,0:T(8,128)} %get-tuple-element.21), kind=kLoop, calls=%fused_computation | loop fusion | flops 589824 | bytes 819200 | tf_op jit(solution)/shard_map/convert_element_type | solution.py:289
Async XLA Ops:
  98.3 26.2 %copy-start = (f32[4,64,128]{2,1,0:T(8,128)S(1)}, f32[4,64,128]{2,1,0:T(8,128)}, u32[]{:S(2)}) copy-start(f32[4,64,128]{2,1,0:T(8,128)} %get-tuple-element.16) | copy-start | bytes 393220

commit v3 on v2

--- a/solution.py
+++ b/solution.py
@@ -10,8 +10,8 @@
 ITERS = 2
 RB_DEV = 16
 MESH = pl.DeviceIdType.MESH
-UNROLL = 64
-CHUNK = 64
+UNROLL = 128
+CHUNK = 128
 
 
 def column_of(row):
@@ -178,6 +178,16 @@
     own[...] = total
     set_ref[group(hi, lo)] = total.astype(jnp.bfloat16)
 
+    def send_squares():
+        squares = jnp.sum(total * total, axis=0)
+        sq_axis[me] = jnp.broadcast_to(row_of(jnp.sum(squares, axis=1, keepdims=True), 128), (8, 128))
+        return [
+            send(sq_axis.at[me], sq_axis.at[me], sqa_send.at[d - 1], sqa_recv.at[d - 1], at((me + d) % n))
+            for d in range(1, n)
+        ]
+
+    if final:
+        sqa_copies = send_squares()
     far_copies = [
         send(set_ref.at[group(hi, lo)], set_ref.at[group(hi, lo)], far_send.at[d], far_recv.at[d], at(order(d) * 2 + lo))
         for d in range(highs - 1)
@@ -187,12 +197,8 @@
         return send(set_ref.at[group(h, lo)], set_ref.at[group(h, lo)], near_send.at[d], near_recv.at[d], at(pair))
 
     near_copies = [to_partner(highs - 1, hi)]
-    squares = jnp.sum(total * total, axis=0)
-    sq_axis[me] = jnp.broadcast_to(row_of(jnp.sum(squares, axis=1, keepdims=True), 128), (8, 128))
-    sqa_copies = [
-        send(sq_axis.at[me], sq_axis.at[me], sqa_send.at[d - 1], sqa_recv.at[d - 1], at((me + d) % n))
-        for d in range(1, n)
-    ]
+    if not final:
+        sqa_copies = send_squares()
 
     def axis_squares():
         for copy in sqa_copies:
@@ -266,10 +272,9 @@
     group_len = RB_DEV // col_devs
     set_blocks = group_len * row_devs
     host_count = RB_DEV * row_devs * tile_side
-    first_block = jnp.zeros((1,), jnp.int32)
-    for r in range(row_devs - 1):
-        first_block = first_block + jnp.where(own_row > r, row_blocks[r:r + 1], 0)
-    live = jnp.arange(tile_slots, dtype=jnp.int32) < tile_count
+    before = jnp.arange(row_devs, dtype=jnp.int32) < own_row
+    first_block = jnp.sum(jnp.where(before, row_blocks, 0))
+    live = jnp.arange(tile_slots, dtype=jnp.int32) < tile_count[0]
     row_slot = tile_rows - first_block
     col_slot = tile_cols // group_len // col_devs * group_len + tile_cols % group_len
     row_pick = jnp.where(live, row_slot, 0)

time: 128 us -> 121 us (0.945)
  between operations: 5.75 us -> 1.33 us
  Pallas kernels: 115 us -> 112 us
  other arithmetic: 5.11 us -> 7.03 us
  local copies, waits for them, and re-layouts: 1.6 us -> 0.01 us
    pallas_call x4, Pallas kernels: 29.4 us -> 26.5 us  [tile_sums(): pl.pallas_call(functools.partial(tiles_kernel, transposed), grid_spec=gri...]
    slice x1 -> x0, local copies, waits for them, and re-layouts: 1.59 us -> none  [local(): first_block = first_block + jnp.where(own_row > r, row_blocks[r:r + 1], 0)]
    reduce_sum x0 -> x1, other arithmetic: none -> 1.29 us  [local(): first_block = jnp.sum(jnp.where(before, row_blocks, 0))]
where the time goes in v3:
time: 121 us; the launch traced here: 120 us
  Pallas kernels  112 us (93%)
  other arithmetic  7.03 us (6%)
  between operations  1.33 us (1%)
    pallas_call x4, Pallas kernels, reduce_set(): pl.pallas_call(functools.partial(reduce_kernel, axis, other, n, m, g, hos...  85.6 us
    pallas_call x4, Pallas kernels, tile_sums(): pl.pallas_call(functools.partial(tiles_kernel, transposed), grid_spec=gri...  26.5 us

profile of v3, /device:TPU:0, one launch (start us, length us, event | category | flops | bytes accessed | tf_op | source)
XLA Modules:
  0.0 120.4 jit_solution(6429370967442447600)
XLA Ops:
  1.3 1.3 %fusion.5 = s32[]{:T(128)} fusion(s32[8]{0:T(128)} %param.11, s32[]{:T(128)S(6)} %axis_index.15), kind=kLoop, calls=%fused_computation.18 | loop fusion | flops 23 | bytes 40 | tf_op jit(solution)/shard_map/reduce_sum | solution.py:276
  2.6 1.9 %fusion.1 = (s32[256]{0:T(256)}, s32[256]{0:T(256)}, s32[256]{0:T(256)}, s32[256]{0:T(256)S(1)}) fusion(s32[256]{0:T(256)} %param.8, s32[]{:T(128)} %fusion.5, s32[]{:T(128)} %bitcast.1, s32[256]{0:T(256)} %param.9), kind=kLoop, calls=%fused_computation.14 | loop fusion | flops 10496 | bytes 6152 | tf_op jit(solution)/shard_map/jit(_where)/select_n | solution.py:282
  4.5 0.5 fusion.3.put_ref
  5.1 6.6 %authority_tiles.2.refs_0_ = bf16[32,64,128]{2,1,0:T(8,128)(2,1)} custom-call(s32[256]{0:T(256)} %get-tuple-element.25.pick_ref, s32[256]{0:T(256)} %fusion.3.put_ref, bf16[24,64,128]{2,1,0:T(8,128)(2,1)} %x_ref.1, bf16[256,128,128]{2,1,0:T(8,128)(2,1)} %tiles_ref.7), custom_call_target="tpu_custom_call" | custom-call | tf_op jit(solution)/shard_map/authority_tiles/pallas_call | solution.py:82
  11.7 27.9 %reduce_row.2 = (bf16[32,64,128]{2,1,0:T(8,128)(2,1)}, f32[8,128]{1,0:T(8,128)}, f32[4,64,128]{2,1,0:T(8,128)}) custom-call(bf16[32,64,128]{2,1,0:T(8,128)(2,1)} %authority_tiles.2.refs_0_), custom_call_target="tpu_custom_call" | custom-call | tf_op jit(solution)/shard_map/reduce_row/pallas_call | solution.py:246
  39.6 6.6 %hub_tiles.2.refs_0_ = bf16[24,64,128]{2,1,0:T(8,128)(2,1)} custom-call(s32[256]{0:T(256)} %get-tuple-element.26.pick_ref, s32[256]{0:T(256)} %get-tuple-element.24.put_ref, bf16[32,64,128]{2,1,0:T(8,128)(2,1)} %get-tuple-element.12.x_ref, bf16[256,128,128]{2,1,0:T(8,128)(2,1)} %tiles_ref.7), custom_call_target="tpu_custom_call" | custom-call | tf_op jit(solution)/shard_map/hub_tiles/pallas_call | solution.py:82
  46.2 13.9 %reduce_col.2 = (bf16[24,64,128]{2,1,0:T(8,128)(2,1)}, f32[8,128]{1,0:T(8,128)}, f32[6,64,128]{2,1,0:T(8,128)}) custom-call(bf16[24,64,128]{2,1,0:T(8,128)(2,1)} %hub_tiles.2.refs_0_, f32[8,128]{1,0:T(8,128)} %get-tuple-element.13.refs_1_), custom_call_target="tpu_custom_call" | custom-call | tf_op jit(solution)/shard_map/reduce_col/pallas_call | solution.py:246
  60.1 6.6 %authority_tiles.3.refs_0_ = bf16[32,64,128]{2,1,0:T(8,128)(2,1)} custom-call(s32[256]{0:T(256)} %get-tuple-element.25.pick_ref, s32[256]{0:T(256)} %fusion.3.put_ref, bf16[24,64,128]{2,1,0:T(8,128)(2,1)} %get-tuple-element.14.x_ref, bf16[256,128,128]{2,1,0:T(8,128)(2,1)} %tiles_ref.7), custom_call_target="tpu_custom_call" | custom-call | tf_op jit(solution)/shard_map/authority_tiles/pallas_call | solution.py:82
  66.7 26.5 %reduce_row.3 = (bf16[32,64,128]{2,1,0:T(8,128)(2,1)}, f32[8,128]{1,0:T(8,128)}, f32[4,64,128]{2,1,0:T(8,128)}) custom-call(bf16[32,64,128]{2,1,0:T(8,128)(2,1)} %authority_tiles.3.refs_0_, f32[8,128]{1,0:T(8,128)} %get-tuple-element.15.refs_1_), custom_call_target="tpu_custom_call" | custom-call | tf_op jit(solution)/shard_map/reduce_row/pallas_call | solution.py:246
  93.3 0.0 copy-start
  93.3 6.7 %hub_tiles.3.refs_0_ = bf16[24,64,128]{2,1,0:T(8,128)(2,1)} custom-call(s32[256]{0:T(256)} %get-tuple-element.26.pick_ref, s32[256]{0:T(256)} %get-tuple-element.24.put_ref, bf16[32,64,128]{2,1,0:T(8,128)(2,1)} %get-tuple-element.17.x_ref, bf16[256,128,128]{2,1,0:T(8,128)(2,1)} %tiles_ref.7), custom_call_target="tpu_custom_call" | custom-call | tf_op jit(solution)/shard_map/hub_tiles/pallas_call | solution.py:82
  100.0 17.2 %reduce_col.3 = (bf16[24,64,128]{2,1,0:T(8,128)(2,1)}, f32[64,128]{1,0:T(8,128)}, f32[64,128]{1,0:T(8,128)}) custom-call(bf16[24,64,128]{2,1,0:T(8,128)(2,1)} %hub_tiles.3.refs_0_, f32[8,128]{1,0:T(8,128)} %get-tuple-element.18.refs_1_), custom_call_target="tpu_custom_call" | custom-call | tf_op jit(solution)/shard_map/reduce_col/pallas_call | solution.py:246
  117.2 0.0 copy-done
  117.2 1.4 %multiply_convert_fusion.1 = bf16[4,64,128]{2,1,0:T(8,128)(2,1)} fusion(f32[4,64,128]{2,1,0:T(8,128)S(1)} %copy-done, f32[64,128]{1,0:T(8,128)} %get-tuple-element.19), kind=kLoop, calls=%fused_computation.1 | loop fusion | flops 65536 | bytes 229376 | tf_op jit(solution)/shard_map/convert_element_type | solution.py:293
  118.6 1.8 %multiply_convert_fusion = bf16[24,64,128]{2,1,0:T(8,128)(2,1)} fusion(bf16[24,64,128]{2,1,0:T(8,128)(2,1)} %get-tuple-element.20, f32[64,128]{1,0:T(8,128)} %get-tuple-element.21), kind=kLoop, calls=%fused_computation | loop fusion | flops 589824 | bytes 819200 | tf_op jit(solution)/shard_map/convert_element_type | solution.py:294
Async XLA Ops:
  93.3 23.9 %copy-start = (f32[4,64,128]{2,1,0:T(8,128)S(1)}, f32[4,64,128]{2,1,0:T(8,128)}, u32[]{:S(2)}) copy-start(f32[4,64,128]{2,1,0:T(8,128)} %get-tuple-element.16) | copy-start | bytes 393220

commit v4 on v3

--- a/solution.py
+++ b/solution.py
@@ -10,8 +10,9 @@
 ITERS = 2
 RB_DEV = 16
 MESH = pl.DeviceIdType.MESH
+MIB = 1 << 20
 UNROLL = 128
-CHUNK = 128
+LIMIT_MIB = 4
 
 
 def column_of(row):
@@ -28,8 +29,10 @@
 
 def tiles_kernel(transposed, pick_ref, put_ref, x_ref, tiles_ref, out_ref, acc):
     step = pl.program_id(0)
-    chunk = tiles_ref.shape[0]
+    chunk = UNROLL
     blocks = out_ref.shape[0]
+    side, k = tiles_ref.shape[1], x_ref.shape[1]
+    base = 0 if tiles_ref.shape[0] == chunk else step * chunk
 
     @pl.when(step == 0)
     def _():
@@ -37,24 +40,18 @@
 
     dims = (((1,), (1,)), ((), ())) if transposed else (((1,), (0,)), ((), ()))
 
-    side = tiles_ref.shape[1]
-    k = x_ref.shape[1]
-
-    @pl.loop(0, chunk // UNROLL)
-    def _(i):
-        products = []
-        for u in range(0, UNROLL, 2):
-            t = i * UNROLL + u
-            x = jnp.concatenate([x_ref[pick_ref[step * chunk + t + v]] for v in range(2)], axis=0)
-            if transposed:
-                both = tiles_ref[pl.ds(t, 2)].reshape(2 * side, side)
-            else:
-                both = jnp.concatenate([tiles_ref[t], tiles_ref[t + 1]], axis=1)
-            product = lax.dot_general(x, both, dims, preferred_element_type=jnp.float32)
-            products += [product[:k, :side], product[k:, side:]]
-        for u in range(UNROLL):
-            where = put_ref[step * chunk + i * UNROLL + u]
-            acc[where] = acc[where] + products[u]
+    products = []
+    for u in range(0, chunk, 2):
+        x = jnp.concatenate([x_ref[pick_ref[step * chunk + u + v]] for v in range(2)], axis=0)
+        if transposed:
+            both = tiles_ref[pl.ds(base + u, 2)].reshape(2 * side, side)
+        else:
+            both = jnp.concatenate([tiles_ref[base + u], tiles_ref[base + u + 1]], axis=1)
+        product = lax.dot_general(x, both, dims, preferred_element_type=jnp.float32)
+        products += [product[:k, :side], product[k:, side:]]
+    for u in range(chunk):
+        where = put_ref[step * chunk + u]
+        acc[where] = acc[where] + products[u]
 
     @pl.when(step == pl.num_programs(0) - 1)
     def _():
@@ -63,26 +60,25 @@
             out_ref[b] = acc[b].astype(jnp.bfloat16)
 
 
-def tile_sums(transposed, blocks, pick, put, x, tiles):
+def tile_sums(transposed, blocks, pick, put, x, tiles, resident):
     slots, side = tiles.shape[0], tiles.shape[1]
     k = x.shape[1]
-    chunk = CHUNK
-    while slots % chunk:
-        chunk //= 2
+    vmem = pl.BlockSpec(memory_space=pltpu.VMEM)
+    held = 2 * UNROLL * side * side * 2
+    streamed = pl.BlockSpec((UNROLL, side, side), lambda i, *_: (i, 0, 0))
     grid_spec = pltpu.PrefetchScalarGridSpec(
         num_scalar_prefetch=2,
-        grid=(slots // chunk,),
-        in_specs=[
-            pl.BlockSpec(x.shape, lambda i, *_: (0, 0, 0)),
-            pl.BlockSpec((chunk, side, side), lambda i, *_: (i, 0, 0)),
-        ],
-        out_specs=pl.BlockSpec((blocks, k, side), lambda i, *_: (0, 0, 0)),
+        grid=(slots // UNROLL,),
+        in_specs=[vmem, vmem if resident else streamed],
+        out_specs=vmem,
         scratch_shapes=[pltpu.VMEM((blocks + 1, k, side), jnp.float32)],
     )
     return pl.pallas_call(
         functools.partial(tiles_kernel, transposed),
         grid_spec=grid_spec,
         out_shape=jax.ShapeDtypeStruct((blocks, k, side), jnp.bfloat16),
+        compiler_params=pltpu.CompilerParams(
+            vmem_limit_bytes=(0 if resident else held) + (x.size + blocks * k * side * 3) * 2 + LIMIT_MIB * MIB),
         name="hub_tiles" if transposed else "authority_tiles",
     )(pick, put, x, tiles)
 
@@ -260,7 +256,8 @@
             dma(highs), dma(highs), dma(highs - 1), dma(highs - 1),
             dma(n - 1), dma(n - 1), dma(n - 1), dma(n - 1), dma(m - 1), dma(m - 1),
         ],
-        compiler_params=pltpu.CompilerParams(collective_id=collective_id, has_side_effects=True),
+        compiler_params=pltpu.CompilerParams(
+            collective_id=collective_id, has_side_effects=True, vmem_limit_bytes=6 * part.size * 2 + 4 * MIB),
         name="reduce_" + axis,
     )(*operands)
 
@@ -284,10 +281,10 @@
     hub, squares = hub_seeds, None
     for iteration in range(ITERS):
         last = iteration == ITERS - 1
-        part = tile_sums(False, set_blocks, row_pick, col_put, hub, tile_blocks)
+        part = tile_sums(False, set_blocks, row_pick, col_put, hub, tile_blocks, True)
         column_set, squares, own = reduce_set(
             "row", "col", row_devs, col_devs, host_count, iteration, False, part, squares)
-        part = tile_sums(True, slot_count, col_pick, row_put, column_set, tile_blocks)
+        part = tile_sums(True, slot_count, col_pick, row_put, column_set, tile_blocks, True)
         hub, squares, rest = reduce_set(
             "col", "row", col_devs, row_devs, host_count, ITERS + iteration, last, part, squares)
     authority = (own * squares[None]).astype(jnp.bfloat16)

time: 121 us -> 103 us (0.85)
  Pallas kernels: 112 us -> 93.3 us
  local copies, waits for them, and re-layouts: 0.01 us -> 4.38 us
  other arithmetic: 7.03 us -> 4.15 us
    pallas_call x4, Pallas kernels: 26.5 us -> 13.8 us  [tile_sums(): pl.pallas_call(functools.partial(tiles_kernel, transposed), grid_spec=gri...]
    pallas_call x4, Pallas kernels: 85.6 us -> 79.5 us  [reduce_set(): pl.pallas_call(functools.partial(reduce_kernel, axis, other, n, m, g, hos...]
    unnamed x2 -> x6, local copies, waits for them, and re-layouts: 0.01 us -> 4.38 us
where the time goes in v4:
time: 103 us
  Pallas kernels  93.3 us (91%)
  local copies, waits for them, and re-layouts  4.38 us (4%)
  other arithmetic  4.15 us (4%)
  between operations  1.37 us (1%)
    pallas_call x4, Pallas kernels, reduce_set(): pl.pallas_call(functools.partial(reduce_kernel, axis, other, n, m, g, hos...  79.5 us
    pallas_call x4, Pallas kernels, tile_sums(): pl.pallas_call(functools.partial(tiles_kernel, transposed), grid_spec=gri...  13.8 us
    unnamed x6, local copies, waits for them, and re-layouts  4.38 us

profile of v4, /device:TPU:0, one launch (start us, length us, event | category | flops | bytes accessed | tf_op | source)
XLA Modules:
  0.0 103.2 jit_solution(1788152084280713362)
XLA Ops:
  1.3 1.3 %fusion.5 = s32[]{:T(128)} fusion(s32[8]{0:T(128)} %param.11, s32[]{:T(128)S(6)} %axis_index.15), kind=kLoop, calls=%fused_computation.18 | loop fusion | flops 23 | bytes 40 | tf_op jit(solution)/shard_map/reduce_sum | solution.py:273
  2.6 1.4 %fusion.1 = (s32[256]{0:T(256)S(1)}, s32[256]{0:T(256)S(1)}, s32[256]{0:T(256)S(1)}, s32[256]{0:T(256)S(1)}) fusion(s32[256]{0:T(256)} %param.8, s32[]{:T(128)} %fusion.5, s32[]{:T(128)} %bitcast.1, s32[256]{0:T(256)} %param.9), kind=kLoop, calls=%fused_computation.14 | loop fusion | flops 10496 | bytes 6152 | tf_op jit(solution)/shard_map/jit(_where)/select_n | solution.py:279
  3.9 0.0 copy-start
  4.0 3.4 %copy-done = bf16[256,128,128]{2,1,0:T(8,128)(2,1)S(1)} copy-done((bf16[256,128,128]{2,1,0:T(8,128)(2,1)S(1)}, bf16[256,128,128]{2,1,0:T(8,128)(2,1)}, u32[]{:S(2)}) %copy-start) | copy-done | bytes 8388632
  7.3 0.0 copy-start.2
  7.3 1.0 copy-done.2
  8.3 0.0 copy-start.1
  8.3 3.5 %authority_tiles.2.refs_0_ = bf16[32,64,128]{2,1,0:T(8,128)(2,1)S(1)} custom-call(s32[256]{0:T(256)S(1)} %get-tuple-element.25.pick_ref, s32[256]{0:T(256)S(1)} %fusion.3.put_ref, bf16[24,64,128]{2,1,0:T(8,128)(2,1)S(1)} %copy-done.2, bf16[256,128,128]{2,1,0:T(8,128)(2,1)S(1)} %copy-done), custom_call_target="tpu_custom_call" | custom-call | tf_op jit(solution)/shard_map/authority_tiles/pallas_call | solution.py:76
  11.8 26.7 %reduce_row.2 = (bf16[32,64,128]{2,1,0:T(8,128)(2,1)S(1)}, f32[8,128]{1,0:T(8,128)S(1)}, f32[4,64,128]{2,1,0:T(8,128)}) custom-call(bf16[32,64,128]{2,1,0:T(8,128)(2,1)S(1)} %authority_tiles.2.refs_0_), custom_call_target="tpu_custom_call" | custom-call | tf_op jit(solution)/shard_map/reduce_row/pallas_call | solution.py:242
  38.6 0.0 copy-done.1
  38.6 3.3 %hub_tiles.2.refs_0_ = bf16[24,64,128]{2,1,0:T(8,128)(2,1)S(1)} custom-call(s32[256]{0:T(256)S(1)} %get-tuple-element.26.pick_ref, s32[256]{0:T(256)S(1)} %get-tuple-element.24.put_ref, bf16[32,64,128]{2,1,0:T(8,128)(2,1)S(1)} %get-tuple-element.12.x_ref, bf16[256,128,128]{2,1,0:T(8,128)(2,1)S(1)} %copy-done.1), custom_call_target="tpu_custom_call" | custom-call | tf_op jit(solution)/shard_map/hub_tiles/pallas_call | solution.py:76
  41.9 13.1 %reduce_col.2 = (bf16[24,64,128]{2,1,0:T(8,128)(2,1)S(1)}, f32[8,128]{1,0:T(8,128)S(1)}, f32[6,64,128]{2,1,0:T(8,128)}) custom-call(bf16[24,64,128]{2,1,0:T(8,128)(2,1)S(1)} %hub_tiles.2.refs_0_, f32[8,128]{1,0:T(8,128)S(1)} %get-tuple-element.13.refs_1_), custom_call_target="tpu_custom_call" | custom-call | tf_op jit(solution)/shard_map/reduce_col/pallas_call | solution.py:242
  55.1 3.5 %authority_tiles.3.refs_0_ = bf16[32,64,128]{2,1,0:T(8,128)(2,1)S(1)} custom-call(s32[256]{0:T(256)S(1)} %get-tuple-element.25.pick_ref, s32[256]{0:T(256)S(1)} %fusion.3.put_ref, bf16[24,64,128]{2,1,0:T(8,128)(2,1)S(1)} %get-tuple-element.14.x_ref, bf16[256,128,128]{2,1,0:T(8,128)(2,1)S(1)} %copy-done.1), custom_call_target="tpu_custom_call" | custom-call | tf_op jit(solution)/shard_map/authority_tiles/pallas_call | solution.py:76
  58.6 23.5 %reduce_row.3 = (bf16[32,64,128]{2,1,0:T(8,128)(2,1)S(1)}, f32[8,128]{1,0:T(8,128)S(1)}, f32[4,64,128]{2,1,0:T(8,128)S(1)}) custom-call(bf16[32,64,128]{2,1,0:T(8,128)(2,1)S(1)} %authority_tiles.3.refs_0_, f32[8,128]{1,0:T(8,128)S(1)} %get-tuple-element.15.refs_1_), custom_call_target="tpu_custom_call" | custom-call | tf_op jit(solution)/shard_map/reduce_row/pallas_call | solution.py:242
  82.1 3.5 %hub_tiles.3.refs_0_ = bf16[24,64,128]{2,1,0:T(8,128)(2,1)S(1)} custom-call(s32[256]{0:T(256)S(1)} %get-tuple-element.26.pick_ref, s32[256]{0:T(256)S(1)} %get-tuple-element.24.put_ref, bf16[32,64,128]{2,1,0:T(8,128)(2,1)S(1)} %get-tuple-element.17.x_ref, bf16[256,128,128]{2,1,0:T(8,128)(2,1)S(1)} %copy-done.1), custom_call_target="tpu_custom_call" | custom-call | tf_op jit(solution)/shard_map/hub_tiles/pallas_call | solution.py:76
  85.6 16.1 %reduce_col.3 = (bf16[24,64,128]{2,1,0:T(8,128)(2,1)S(1)}, f32[64,128]{1,0:T(8,128)S(1)}, f32[64,128]{1,0:T(8,128)S(1)}) custom-call(bf16[24,64,128]{2,1,0:T(8,128)(2,1)S(1)} %hub_tiles.3.refs_0_, f32[8,128]{1,0:T(8,128)S(1)} %get-tuple-element.18.refs_1_), custom_call_target="tpu_custom_call" | custom-call | tf_op jit(solution)/shard_map/reduce_col/pallas_call | solution.py:242
  101.7 0.6 multiply_convert_fusion.1
  102.4 0.8 multiply_convert_fusion
  (1 shorter events, 0.0 us)
Async XLA Ops:
  3.9 3.4 %copy-start = (bf16[256,128,128]{2,1,0:T(8,128)(2,1)S(1)}, bf16[256,128,128]{2,1,0:T(8,128)(2,1)}, u32[]{:S(2)}) copy-start(bf16[256,128,128]{2,1,0:T(8,128)(2,1)} %tiles_ref.7) | copy-start | bytes 25165828
  7.3 1.0 copy-start.2
  8.3 30.2 %copy-start.1 = (bf16[256,128,128]{2,1,0:T(8,128)(2,1)S(1)}, bf16[256,128,128]{2,1,0:T(8,128)(2,1)}, u32[]{:S(2)}) copy-start(bf16[256,128,128]{2,1,0:T(8,128)(2,1)} %tiles_ref.7) | copy-start | bytes 25165828

commit v5 on v4

--- a/solution.py
+++ b/solution.py
@@ -88,6 +88,10 @@
     return jnp.broadcast_to(column_of(row[0:1, :k]), (k, side))
 
 
+def parts_of(g):
+    return 2 if g % 2 == 0 else 1
+
+
 def reduce_kernel(axis, other, n, m, g, hosts, scaled, final, *refs):
     refs = list(refs)
     part_ref = refs.pop(0)
@@ -134,12 +138,22 @@
     def group(h, l):
         return pl.ds((h * 2 + l) * g, g)
 
+    parts = parts_of(g)
+    width = g // parts
+
+    def part_of(h, l, c):
+        return pl.ds((h * 2 + l) * g + c * width, width)
+
+    def piece(c):
+        return pl.ds(c * width, width)
+
     def order(d):
         return (hi + 1 + d) % highs
 
     pair_copies = [
-        send(part_ref.at[group(order(d), 1 - lo)], pair_in.at[d], pair_send.at[d], pair_recv.at[d], at(pair))
-        for d in range(highs)
+        send(part_ref.at[part_of(order(d), 1 - lo, c)], pair_in.at[d, piece(c)],
+             pair_send.at[d * parts + c], pair_recv.at[d * parts + c], at(pair))
+        for d in range(highs) for c in range(parts)
     ]
     sqb_copies = []
     if scaled:
@@ -151,13 +165,17 @@
     hop_copies = []
     for d in range(highs):
         h = order(d)
-        pair_copies[d].wait_recv()
-        total = part_ref[group(h, lo)].astype(jnp.float32) + pair_in[d].astype(jnp.float32)
-        if d == highs - 1:
-            own[...] = total
-        else:
-            hop_out[d] = total.astype(jnp.bfloat16)
-            hop_copies.append(send(hop_out.at[d], hop_in.at[d], hop_send.at[d], hop_recv.at[d], at(h * 2 + lo)))
+        for c in range(parts):
+            at_sem = d * parts + c
+            pair_copies[at_sem].wait_recv()
+            total = part_ref[part_of(h, lo, c)].astype(jnp.float32) + pair_in[d, piece(c)].astype(jnp.float32)
+            if d == highs - 1:
+                own[piece(c)] = total
+            else:
+                hop_out[d, piece(c)] = total.astype(jnp.bfloat16)
+                hop_copies.append(send(
+                    hop_out.at[d, piece(c)], hop_in.at[d, piece(c)],
+                    hop_send.at[at_sem], hop_recv.at[at_sem], at(h * 2 + lo)))
     if scaled:
         for copy in sqb_copies:
             copy.wait_recv()
@@ -184,15 +202,21 @@
 
     if final:
         sqa_copies = send_squares()
-    far_copies = [
-        send(set_ref.at[group(hi, lo)], set_ref.at[group(hi, lo)], far_send.at[d], far_recv.at[d], at(order(d) * 2 + lo))
-        for d in range(highs - 1)
-    ]
-
-    def to_partner(d, h):
-        return send(set_ref.at[group(h, lo)], set_ref.at[group(h, lo)], near_send.at[d], near_recv.at[d], at(pair))
-
-    near_copies = [to_partner(highs - 1, hi)]
+    far_copies = {}
+
+    def to_partner(d, h, c):
+        where = part_of(h, lo, c)
+        at_sem = d * parts + c
+        return send(set_ref.at[where], set_ref.at[where], near_send.at[at_sem], near_recv.at[at_sem], at(pair))
+
+    near_copies = []
+    for c in range(parts):
+        where = part_of(hi, lo, c)
+        for d in range(highs - 1):
+            at_sem = d * parts + c
+            far_copies[d, c] = send(
+                set_ref.at[where], set_ref.at[where], far_send.at[at_sem], far_recv.at[at_sem], at(order(d) * 2 + lo))
+        near_copies.append(to_partner(highs - 1, hi, c))
     if not final:
         sqa_copies = send_squares()
 
@@ -208,9 +232,10 @@
             send(sq_other.at[mo], sq_other.at[mo], sqo_send.at[d - 1], sqo_recv.at[d - 1], {axis: me, other: (mo + d) % m})
             for d in range(1, m)
         ]
-    for d in range(highs - 1):
-        far_copies[d].wait_recv()
-        near_copies.append(to_partner(d, (hi + highs - 1 - d) % highs))
+    for c in range(parts):
+        for d in range(highs - 1):
+            far_copies[d, c].wait_recv()
+            near_copies.append(to_partner(d, (hi + highs - 1 - d) % highs, c))
     if final:
         for copy in sqo_copies:
             copy.wait_recv()
@@ -252,8 +277,7 @@
             pltpu.VMEM((n, 8, 128), jnp.float32),
             pltpu.VMEM((m, 8, 128), jnp.float32),
             *scratch,
-            dma(highs), dma(highs), dma(highs - 1), dma(highs - 1),
-            dma(highs), dma(highs), dma(highs - 1), dma(highs - 1),
+            *[dma(count * parts_of(g)) for count in (highs, highs, highs - 1, highs - 1) * 2],
             dma(n - 1), dma(n - 1), dma(n - 1), dma(n - 1), dma(m - 1), dma(m - 1),
         ],
         compiler_params=pltpu.CompilerParams(

time: 103 us -> 102 us (level)
  Pallas kernels: 93.3 us -> 91.6 us
    pallas_call x4, Pallas kernels: 79.5 us -> 77.4 us  [reduce_set(): pl.pallas_call(functools.partial(reduce_kernel, axis, other, n, m, g, hos...]
where the time goes in v5:
time: 102 us; the launch traced here: 101 us
  Pallas kernels  91.6 us (90%)
  local copies, waits for them, and re-layouts  4.38 us (4%)
  other arithmetic  4.15 us (4%)
  between operations  1.37 us (1%)
    pallas_call x4, Pallas kernels, reduce_set(): pl.pallas_call(functools.partial(reduce_kernel, axis, other, n, m, g, hos...  77.4 us
    pallas_call x4, Pallas kernels, tile_sums(): pl.pallas_call(functools.partial(tiles_kernel, transposed), grid_spec=gri...  14.1 us
    unnamed x6, local copies, waits for them, and re-layouts  4.38 us

profile of v5, /device:TPU:0, one launch (start us, length us, event | category | flops | bytes accessed | tf_op | source)
XLA Modules:
  0.0 101.5 jit_solution(9428933423428951038)
XLA Ops:
  1.3 1.3 %fusion.5 = s32[]{:T(128)} fusion(s32[8]{0:T(128)} %param.11, s32[]{:T(128)S(6)} %axis_index.15), kind=kLoop, calls=%fused_computation.18 | loop fusion | flops 23 | bytes 40 | tf_op jit(solution)/shard_map/reduce_sum | solution.py:297
  2.6 1.4 %fusion.1 = (s32[256]{0:T(256)S(1)}, s32[256]{0:T(256)S(1)}, s32[256]{0:T(256)S(1)}, s32[256]{0:T(256)S(1)}) fusion(s32[256]{0:T(256)} %param.8, s32[]{:T(128)} %fusion.5, s32[]{:T(128)} %bitcast.1, s32[256]{0:T(256)} %param.9), kind=kLoop, calls=%fused_computation.14 | loop fusion | flops 10496 | bytes 6152 | tf_op jit(solution)/shard_map/jit(_where)/select_n | solution.py:303
  3.9 0.0 copy-start
  4.0 3.4 %copy-done = bf16[256,128,128]{2,1,0:T(8,128)(2,1)S(1)} copy-done((bf16[256,128,128]{2,1,0:T(8,128)(2,1)S(1)}, bf16[256,128,128]{2,1,0:T(8,128)(2,1)}, u32[]{:S(2)}) %copy-start) | copy-done | bytes 8388632
  7.3 0.0 copy-start.2
  7.3 1.0 copy-done.2
  8.3 0.0 copy-start.1
  8.3 3.6 %authority_tiles.2.refs_0_ = bf16[32,64,128]{2,1,0:T(8,128)(2,1)S(1)} custom-call(s32[256]{0:T(256)S(1)} %get-tuple-element.25.pick_ref, s32[256]{0:T(256)S(1)} %fusion.3.put_ref, bf16[24,64,128]{2,1,0:T(8,128)(2,1)S(1)} %copy-done.2, bf16[256,128,128]{2,1,0:T(8,128)(2,1)S(1)} %copy-done), custom_call_target="tpu_custom_call" | custom-call | tf_op jit(solution)/shard_map/authority_tiles/pallas_call | solution.py:76
  11.9 26.7 %reduce_row.2 = (bf16[32,64,128]{2,1,0:T(8,128)(2,1)S(1)}, f32[8,128]{1,0:T(8,128)S(1)}, f32[4,64,128]{2,1,0:T(8,128)}) custom-call(bf16[32,64,128]{2,1,0:T(8,128)(2,1)S(1)} %authority_tiles.2.refs_0_), custom_call_target="tpu_custom_call" | custom-call | tf_op jit(solution)/shard_map/reduce_row/pallas_call | solution.py:267
  38.6 0.0 copy-done.1
  38.6 3.4 %hub_tiles.2.refs_0_ = bf16[24,64,128]{2,1,0:T(8,128)(2,1)S(1)} custom-call(s32[256]{0:T(256)S(1)} %get-tuple-element.26.pick_ref, s32[256]{0:T(256)S(1)} %get-tuple-element.24.put_ref, bf16[32,64,128]{2,1,0:T(8,128)(2,1)S(1)} %get-tuple-element.12.x_ref, bf16[256,128,128]{2,1,0:T(8,128)(2,1)S(1)} %copy-done.1), custom_call_target="tpu_custom_call" | custom-call | tf_op jit(solution)/shard_map/hub_tiles/pallas_call | solution.py:76
  42.1 12.6 %reduce_col.2 = (bf16[24,64,128]{2,1,0:T(8,128)(2,1)S(1)}, f32[8,128]{1,0:T(8,128)S(1)}, f32[6,64,128]{2,1,0:T(8,128)}) custom-call(bf16[24,64,128]{2,1,0:T(8,128)(2,1)S(1)} %hub_tiles.2.refs_0_, f32[8,128]{1,0:T(8,128)S(1)} %get-tuple-element.13.refs_1_), custom_call_target="tpu_custom_call" | custom-call | tf_op jit(solution)/shard_map/reduce_col/pallas_call | solution.py:267
  54.7 3.6 %authority_tiles.3.refs_0_ = bf16[32,64,128]{2,1,0:T(8,128)(2,1)S(1)} custom-call(s32[256]{0:T(256)S(1)} %get-tuple-element.25.pick_ref, s32[256]{0:T(256)S(1)} %fusion.3.put_ref, bf16[24,64,128]{2,1,0:T(8,128)(2,1)S(1)} %get-tuple-element.14.x_ref, bf16[256,128,128]{2,1,0:T(8,128)(2,1)S(1)} %copy-done.1), custom_call_target="tpu_custom_call" | custom-call | tf_op jit(solution)/shard_map/authority_tiles/pallas_call | solution.py:76
  58.3 22.9 %reduce_row.3 = (bf16[32,64,128]{2,1,0:T(8,128)(2,1)S(1)}, f32[8,128]{1,0:T(8,128)S(1)}, f32[4,64,128]{2,1,0:T(8,128)S(1)}) custom-call(bf16[32,64,128]{2,1,0:T(8,128)(2,1)S(1)} %authority_tiles.3.refs_0_, f32[8,128]{1,0:T(8,128)S(1)} %get-tuple-element.15.refs_1_), custom_call_target="tpu_custom_call" | custom-call | tf_op jit(solution)/shard_map/reduce_row/pallas_call | solution.py:267
  81.2 3.6 %hub_tiles.3.refs_0_ = bf16[24,64,128]{2,1,0:T(8,128)(2,1)S(1)} custom-call(s32[256]{0:T(256)S(1)} %get-tuple-element.26.pick_ref, s32[256]{0:T(256)S(1)} %get-tuple-element.24.put_ref, bf16[32,64,128]{2,1,0:T(8,128)(2,1)S(1)} %get-tuple-element.17.x_ref, bf16[256,128,128]{2,1,0:T(8,128)(2,1)S(1)} %copy-done.1), custom_call_target="tpu_custom_call" | custom-call | tf_op jit(solution)/shard_map/hub_tiles/pallas_call | solution.py:76
  84.8 15.2 %reduce_col.3 = (bf16[24,64,128]{2,1,0:T(8,128)(2,1)S(1)}, f32[64,128]{1,0:T(8,128)S(1)}, f32[64,128]{1,0:T(8,128)S(1)}) custom-call(bf16[24,64,128]{2,1,0:T(8,128)(2,1)S(1)} %hub_tiles.3.refs_0_, f32[8,128]{1,0:T(8,128)S(1)} %get-tuple-element.18.refs_1_), custom_call_target="tpu_custom_call" | custom-call | tf_op jit(solution)/shard_map/reduce_col/pallas_call | solution.py:267
  100.0 0.6 multiply_convert_fusion.1
  100.6 0.8 multiply_convert_fusion
  (1 shorter events, 0.0 us)
Async XLA Ops:
  3.9 3.4 %copy-start = (bf16[256,128,128]{2,1,0:T(8,128)(2,1)S(1)}, bf16[256,128,128]{2,1,0:T(8,128)(2,1)}, u32[]{:S(2)}) copy-start(bf16[256,128,128]{2,1,0:T(8,128)(2,1)} %tiles_ref.7) | copy-start | bytes 25165828
  7.3 1.0 copy-start.2
  8.3 30.3 %copy-start.1 = (bf16[256,128,128]{2,1,0:T(8,128)(2,1)S(1)}, bf16[256,128,128]{2,1,0:T(8,128)(2,1)}, u32[]{:S(2)}) copy-start(bf16[256,128,128]{2,1,0:T(8,128)(2,1)} %tiles_ref.7) | copy-start | bytes 25165828

commit v6 on v5

--- a/solution.py
+++ b/solution.py
@@ -89,7 +89,7 @@
 
 
 def parts_of(g):
-    return 2 if g % 2 == 0 else 1
+    return 4 if g % 4 == 0 else 2 if g % 2 == 0 else 1
 
 
 def reduce_kernel(axis, other, n, m, g, hosts, scaled, final, *refs):

time: 102 us -> 102 us (level)
  no operation moved by 1% of the time
where the time goes in v6:
time: 102 us
  Pallas kernels  91.9 us (90%)
  local copies, waits for them, and re-layouts  4.38 us (4%)
  other arithmetic  4.15 us (4%)
  between operations  1.37 us (1%)
    pallas_call x4, Pallas kernels, reduce_set(): pl.pallas_call(functools.partial(reduce_kernel, axis, other, n, m, g, hos...  77.8 us
    pallas_call x4, Pallas kernels, tile_sums(): pl.pallas_call(functools.partial(tiles_kernel, transposed), grid_spec=gri...  14.1 us
    unnamed x6, local copies, waits for them, and re-layouts  4.38 us

profile of v6, /device:TPU:0, one launch (start us, length us, event | category | flops | bytes accessed | tf_op | source)
XLA Modules:
  0.0 101.8 jit_solution(2568555600880220842)
XLA Ops:
  1.3 1.3 %fusion.5 = s32[]{:T(128)} fusion(s32[8]{0:T(128)} %param.11, s32[]{:T(128)S(6)} %axis_index.15), kind=kLoop, calls=%fused_computation.18 | loop fusion | flops 23 | bytes 40 | tf_op jit(solution)/shard_map/reduce_sum | solution.py:297
  2.6 1.4 %fusion.1 = (s32[256]{0:T(256)S(1)}, s32[256]{0:T(256)S(1)}, s32[256]{0:T(256)S(1)}, s32[256]{0:T(256)S(1)}) fusion(s32[256]{0:T(256)} %param.8, s32[]{:T(128)} %fusion.5, s32[]{:T(128)} %bitcast.1, s32[256]{0:T(256)} %param.9), kind=kLoop, calls=%fused_computation.14 | loop fusion | flops 10496 | bytes 6152 | tf_op jit(solution)/shard_map/jit(_where)/select_n | solution.py:303
  3.9 0.0 copy-start
  4.0 3.4 %copy-done = bf16[256,128,128]{2,1,0:T(8,128)(2,1)S(1)} copy-done((bf16[256,128,128]{2,1,0:T(8,128)(2,1)S(1)}, bf16[256,128,128]{2,1,0:T(8,128)(2,1)}, u32[]{:S(2)}) %copy-start) | copy-done | bytes 8388632
  7.3 0.0 copy-start.2
  7.3 1.0 copy-done.2
  8.3 0.0 copy-start.1
  8.3 3.6 %authority_tiles.2.refs_0_ = bf16[32,64,128]{2,1,0:T(8,128)(2,1)S(1)} custom-call(s32[256]{0:T(256)S(1)} %get-tuple-element.25.pick_ref, s32[256]{0:T(256)S(1)} %fusion.3.put_ref, bf16[24,64,128]{2,1,0:T(8,128)(2,1)S(1)} %copy-done.2, bf16[256,128,128]{2,1,0:T(8,128)(2,1)S(1)} %copy-done), custom_call_target="tpu_custom_call" | custom-call | tf_op jit(solution)/shard_map/authority_tiles/pallas_call | solution.py:76
  11.9 26.9 %reduce_row.2 = (bf16[32,64,128]{2,1,0:T(8,128)(2,1)S(1)}, f32[8,128]{1,0:T(8,128)S(1)}, f32[4,64,128]{2,1,0:T(8,128)}) custom-call(bf16[32,64,128]{2,1,0:T(8,128)(2,1)S(1)} %authority_tiles.2.refs_0_), custom_call_target="tpu_custom_call" | custom-call | tf_op jit(solution)/shard_map/reduce_row/pallas_call | solution.py:267
  38.8 0.0 copy-done.1
  38.8 3.4 %hub_tiles.2.refs_0_ = bf16[24,64,128]{2,1,0:T(8,128)(2,1)S(1)} custom-call(s32[256]{0:T(256)S(1)} %get-tuple-element.26.pick_ref, s32[256]{0:T(256)S(1)} %get-tuple-element.24.put_ref, bf16[32,64,128]{2,1,0:T(8,128)(2,1)S(1)} %get-tuple-element.12.x_ref, bf16[256,128,128]{2,1,0:T(8,128)(2,1)S(1)} %copy-done.1), custom_call_target="tpu_custom_call" | custom-call | tf_op jit(solution)/shard_map/hub_tiles/pallas_call | solution.py:76
  42.2 12.6 %reduce_col.2 = (bf16[24,64,128]{2,1,0:T(8,128)(2,1)S(1)}, f32[8,128]{1,0:T(8,128)S(1)}, f32[6,64,128]{2,1,0:T(8,128)}) custom-call(bf16[24,64,128]{2,1,0:T(8,128)(2,1)S(1)} %hub_tiles.2.refs_0_, f32[8,128]{1,0:T(8,128)S(1)} %get-tuple-element.13.refs_1_), custom_call_target="tpu_custom_call" | custom-call | tf_op jit(solution)/shard_map/reduce_col/pallas_call | solution.py:267
  54.9 3.5 %authority_tiles.3.refs_0_ = bf16[32,64,128]{2,1,0:T(8,128)(2,1)S(1)} custom-call(s32[256]{0:T(256)S(1)} %get-tuple-element.25.pick_ref, s32[256]{0:T(256)S(1)} %fusion.3.put_ref, bf16[24,64,128]{2,1,0:T(8,128)(2,1)S(1)} %get-tuple-element.14.x_ref, bf16[256,128,128]{2,1,0:T(8,128)(2,1)S(1)} %copy-done.1), custom_call_target="tpu_custom_call" | custom-call | tf_op jit(solution)/shard_map/authority_tiles/pallas_call | solution.py:76
  58.4 23.2 %reduce_row.3 = (bf16[32,64,128]{2,1,0:T(8,128)(2,1)S(1)}, f32[8,128]{1,0:T(8,128)S(1)}, f32[4,64,128]{2,1,0:T(8,128)S(1)}) custom-call(bf16[32,64,128]{2,1,0:T(8,128)(2,1)S(1)} %authority_tiles.3.refs_0_, f32[8,128]{1,0:T(8,128)S(1)} %get-tuple-element.15.refs_1_), custom_call_target="tpu_custom_call" | custom-call | tf_op jit(solution)/shard_map/reduce_row/pallas_call | solution.py:267
  81.6 3.6 %hub_tiles.3.refs_0_ = bf16[24,64,128]{2,1,0:T(8,128)(2,1)S(1)} custom-call(s32[256]{0:T(256)S(1)} %get-tuple-element.26.pick_ref, s32[256]{0:T(256)S(1)} %get-tuple-element.24.put_ref, bf16[32,64,128]{2,1,0:T(8,128)(2,1)S(1)} %get-tuple-element.17.x_ref, bf16[256,128,128]{2,1,0:T(8,128)(2,1)S(1)} %copy-done.1), custom_call_target="tpu_custom_call" | custom-call | tf_op jit(solution)/shard_map/hub_tiles/pallas_call | solution.py:76
  85.2 15.0 %reduce_col.3 = (bf16[24,64,128]{2,1,0:T(8,128)(2,1)S(1)}, f32[64,128]{1,0:T(8,128)S(1)}, f32[64,128]{1,0:T(8,128)S(1)}) custom-call(bf16[24,64,128]{2,1,0:T(8,128)(2,1)S(1)} %hub_tiles.3.refs_0_, f32[8,128]{1,0:T(8,128)S(1)} %get-tuple-element.18.refs_1_), custom_call_target="tpu_custom_call" | custom-call | tf_op jit(solution)/shard_map/reduce_col/pallas_call | solution.py:267
  100.3 0.6 multiply_convert_fusion.1
  100.9 0.8 multiply_convert_fusion
  (1 shorter events, 0.0 us)
Async XLA Ops:
  3.9 3.4 %copy-start = (bf16[256,128,128]{2,1,0:T(8,128)(2,1)S(1)}, bf16[256,128,128]{2,1,0:T(8,128)(2,1)}, u32[]{:S(2)}) copy-start(bf16[256,128,128]{2,1,0:T(8,128)(2,1)} %tiles_ref.7) | copy-start | bytes 25165828
  7.3 1.0 copy-start.2
  8.3 30.5 %copy-start.1 = (bf16[256,128,128]{2,1,0:T(8,128)(2,1)S(1)}, bf16[256,128,128]{2,1,0:T(8,128)(2,1)}, u32[]{:S(2)}) copy-start(bf16[256,128,128]{2,1,0:T(8,128)(2,1)} %tiles_ref.7) | copy-start | bytes 25165828
